TPU v7x, 16 devices: a whole 2x2x2 slice. The times are simulated.
16 devices in a mesh: outer: 2 (over z), middle: 2 (over y), inner: 4 (over x, core).
Axes of the slice: x: 2, y: 2, z: 2, core: 2. Of those that a mesh axis runs over, the one named last changes fastest.
Arguments:
- g_embed: float32 [16, 4096, 1024], P(('outer', 'middle', 'inner'))
- g_attn: float32 [16, 1, 1024, 4096], P(('outer', 'middle', 'inner'))
- g_ffn_in: float32 [16, 1, 1024, 2816], P(('outer', 'middle', 'inner'))
- g_ffn_out: float32 [16, 1, 2816, 1024], P(('outer', 'middle', 'inner'))
- g_vec: float32 [16, 1, 12032], P(('outer', 'middle', 'inner'))
- m_flat: float32 [14167808], P(('outer', 'middle', 'inner'))
- v_flat: float32 [14167808], P(('outer', 'middle', 'inner'))
- w_flat: float32 [14167808], P(('outer', 'middle', 'inner'))
Outputs:
- output 1: float32 [14167808], P(('outer', 'middle', 'inner'))
- output 2: float32 [14167808], P(('outer', 'middle', 'inner'))
- output 3: float32 [14167808], P(('outer', 'middle', 'inner'))
- output 4: bfloat16 [4096, 1024], replicated
- output 5: bfloat16 [1, 1024, 4096], replicated
- output 6: bfloat16 [1, 1024, 2816], replicated
- output 7: bfloat16 [1, 2816, 1024], replicated
- output 8: bfloat16 [1, 12032], replicated
- output 9: bfloat16 [16, 1770976], P(('outer', 'middle', 'inner'))
All inputs are finite; a program needn't handle non-finite values.
Results may differ from a plain program's by a relative error of at most 0.001.
Values are sent between devices in bfloat16 or wider.
A program may use at most 1 GiB of HBM per device.

v0:
```python
import math
import jax
import jax.numpy as jnp
from jax import lax
from jax.sharding import PartitionSpec as P

MESH_AXES = ('outer', 'middle', 'inner')
ADAM_BETA1 = 0.9
ADAM_BETA2 = 0.98
ADAM_EPS = 1e-9
LEARN_RATE = 0.05
ADAM_STEP = 3


def adam_update(grad_mean, m_old, v_old, w_old):
    m_new = ADAM_BETA1 * m_old + (1.0 - ADAM_BETA1) * grad_mean
    v_new = ADAM_BETA2 * v_old + (1.0 - ADAM_BETA2) * (grad_mean * grad_mean)
    m_hat = m_new / (1.0 - ADAM_BETA1 ** ADAM_STEP)
    v_hat = v_new / (1.0 - ADAM_BETA2 ** ADAM_STEP)
    w_new = w_old - LEARN_RATE * m_hat / (jnp.sqrt(v_hat) + ADAM_EPS)
    return m_new, v_new, w_new


def split_tensors(flat_values, shape_list):
    pieces = []
    offset = 0
    for shape in shape_list:
        count = math.prod(shape)
        pieces.append(flat_values[offset:offset + count].reshape(shape))
        offset += count
    return pieces


def own_chip_block(w_tensors, chip_index, num_chips):
    embed_rows = w_tensors[0].shape[0] // num_chips
    block_list = [lax.dynamic_slice_in_dim(w_tensors[0], chip_index * embed_rows, embed_rows, axis=0).reshape(-1)]
    for tensor in w_tensors[1:]:
        block_rows = tensor.shape[1] // num_chips
        block_list.append(lax.dynamic_slice_in_dim(tensor, chip_index * block_rows, block_rows, axis=1).reshape(-1))
    return jnp.concatenate(block_list)[None, :]


def solution(mesh):
    num_devices = mesh.shape['outer'] * mesh.shape['middle'] * mesh.shape['inner']
    num_chips = num_devices // 2

    def local_step(g_embed, g_attn, g_ffn_in, g_ffn_out, g_vec, m_shard, v_shard, w_shard):
        grad_list = (g_embed, g_attn, g_ffn_in, g_ffn_out, g_vec)
        local_flat = jnp.concatenate([gradient.reshape(-1) for gradient in grad_list])
        grad_mean = lax.psum_scatter(local_flat, MESH_AXES, scatter_dimension=0, tiled=True) / num_devices
        m_new, v_new, w_new = adam_update(grad_mean, m_shard, v_shard, w_shard)
        w_full = lax.all_gather(w_new.astype(jnp.bfloat16), MESH_AXES, axis=0, tiled=True)
        w_tensors = split_tensors(w_full, [gradient.shape[1:] for gradient in grad_list])
        device_index = (lax.axis_index('outer') * mesh.shape['middle'] + lax.axis_index('middle')) * mesh.shape['inner'] + lax.axis_index('inner')
        w_chip = own_chip_block(w_tensors, device_index // 2, num_chips)
        return (m_new, v_new, w_new) + tuple(w_tensors) + (w_chip,)

    return jax.shard_map(local_step, mesh=mesh, in_specs=(P(MESH_AXES),) * 8, out_specs=(P(MESH_AXES),) * 3 + (P(),) * 5 + (P(MESH_AXES),), check_vma=False)
```

profile of v0, /device:TPU:0, one launch (start us, length us, event | category | flops | bytes accessed | tf_op | source)
XLA Modules:
  0.0 1043.1 jit_solution(12824743380538956459)
XLA Ops:
  7.2 0.0 all-reduce.7.cloned.1.call-start
  7.2 0.0 slice-start.6
  7.2 0.0 slice-start.7
  7.2 10.2 copy.17
  17.4 0.0 slice-start.8
  17.4 0.0 slice-start.9
  17.4 8.1 constant_dynamic-update-slice_fusion
  25.5 0.0 slice-done.6
  25.5 0.0 slice-done.7
  25.5 0.0 slice-done.8
  25.5 0.4 slice-done.9
  26.0 7.1 copy.18
  33.0 12.6 %reshape.67 = f32[2883584]{0:T(1024)} reshape(f32[1,1,1024,2816]{3,2,1,0:T(8,128)} %param.10) | data formatting | bytes 23068672 | tf_op jit(solution)/shard_map/reshape | solution.py:49
  45.6 0.0 slice-start.3
  45.6 0.0 slice-start.4
  45.6 11.7 %copy.19 = f32[352,8,8,128]{3,1,2,0:T(8,128)} copy(f32[352,8,8,128]{3,2,1,0:T(8,128)} %bitcast.28) | data formatting | bytes 23068672
  57.4 0.0 slice-start.5
  57.4 0.0 slice-start
  57.4 0.0 slice-start.1
  57.4 13.2 %constant_dynamic-update-slice_fusion.5 = f32[14167808]{0:T(1024)} fusion(f32[14167808]{0:T(1024)} %constant_dynamic-update-slice_fusion, f32[4194304]{0:T(1024)} %bitcast.17), kind=kLoop, calls=%fused_computation.11 | loop fusion | bytes 33554432
  70.6 0.0 slice-done.3
  70.6 0.0 slice-done.4
  70.6 0.0 slice-done.5
  70.6 0.0 slice-start.2
  70.6 5.9 constant_dynamic-update-slice_fusion.4
  76.5 0.0 slice-done
  76.5 0.0 slice-done.1
  76.5 1.3 slice-done.2
  77.8 0.0 copy-start.1
  77.8 4.5 constant_dynamic-update-slice_fusion.3
  82.3 0.0 copy-done.1
  82.3 0.1 reduce
  82.4 0.6 constant_dynamic-update-slice_fusion.2
  83.0 0.0 all-reduce.7.cloned.1.call-update
  83.0 0.2 all-reduce.5.cloned.1.call-start
  83.3 507.0 %all-reduce.7.cloned.1.call-done = f32[14167808]{0:T(1024)} async-done(((f32[14167808]{0:T(1024)}), f32[14167808]{0:T(1024)}) %all-reduce.7.cloned.1.call-update) | async-done | bytes 56671248
  590.3 8.9 fusion
  599.2 9.3 broadcast.6
  608.6 27.8 %dynamic-update-slice = bf16[14167808]{0:T(1024)(128)(2,1)} dynamic-update-slice(bf16[14167808]{0:T(1024)(128)(2,1)} %broadcast.6, bf16[885488]{0:T(1024)(128)(2,1)S(1)} %get-tuple-element.9, u32[]{:T(128)S(6)} %multiply.8) | dynamic-update-slice | bytes 3541956
  636.3 0.0 all-reduce.5.cloned.1.call-update
  636.4 274.5 %all-reduce.5.cloned.1.call-done = bf16[14167808]{0:T(1024)(128)(2,1)} async-done(((bf16[14167808]{0:T(1024)(128)(2,1)}), bf16[14167808]{0:T(1024)(128)(2,1)}) %all-reduce.5.cloned.1.call-update) | async-done | bytes 28335632
  910.9 11.4 %fusion.2 = (bf16[4194304]{0:T(1024)(128)(2,1)}, bf16[4194304]{0:T(1024)(128)(2,1)}) fusion(bf16[14167808]{0:T(1024)(128)(2,1)} %all-reduce.5.cloned.1.call-done), kind=kLoop, calls=%fused_computation.19 | loop fusion | bytes 33554432 | tf_op jit(solution)/shard_map/slice | solution.py:29
  922.4 13.3 %reshape.70 = bf16[4096,1024]{1,0:T(8,128)(2,1)} reshape(bf16[4194304]{0:T(1024)(128)(2,1)} %get-tuple-element.16) | data formatting | bytes 16777216 | tf_op jit(solution)/shard_map/reshape | solution.py:29
  935.6 13.3 %reshape.71 = bf16[1,1024,4096]{2,1,0:T(8,128)(2,1)} reshape(bf16[4194304]{0:T(1024)(128)(2,1)} %get-tuple-element.15) | data formatting | bytes 16777216 | tf_op jit(solution)/shard_map/reshape | solution.py:29
  948.9 9.5 fusion.1
  958.4 11.5 %reshape.72 = bf16[1,1024,2816]{2,1,0:T(8,128)(2,1)} reshape(bf16[2883584]{0:T(1024)(128)(2,1)} %get-tuple-element.14) | data formatting | bytes 11534336 | tf_op jit(solution)/shard_map/reshape | solution.py:29
  969.9 9.7 reshape.73
  979.6 0.7 slice.24
  980.3 0.0 copy-start
  980.4 0.6 copy-done
  981.0 0.6 reshape.74
  981.6 1.3 dynamic-slice_bitcast_fusion.1
  982.9 0.3 copy.20
  983.2 0.1 constant_dynamic-update-slice_fusion.1
  983.3 1.3 dynamic-slice_bitcast_fusion
  984.6 1.2 copy.21
  985.8 2.0 constant_dynamic-slice_fusion
  987.8 2.7 reshape.77
  990.5 1.2 dynamic-slice_bitcast_fusion.2
  991.6 0.1 copy.22
  991.8 1.3 constant_dynamic-update-slice_fusion.9
  993.1 1.2 constant_dynamic-update-slice_fusion.8
  994.3 0.8 constant_dynamic-update-slice_fusion.6
  995.1 41.2 %broadcast_in_dim.3 = bf16[1,1770976]{1,0:T(2,128)(2,1)} reshape(bf16[1770976]{0:T(1024)(128)(2,1)S(1)} %constant_dynamic-update-slice_fusion.6) | data formatting | bytes 7083904 | tf_op jit(solution)/shard_map/broadcast_in_dim | solution.py:40
  (4 shorter events, 0.1 us)
Async XLA Ops:
  7.2 583.1 %all-reduce.7.cloned.1.call-start = ((), (), s32[]{:S(2)}) async-start(), calls=%async_computation.1 | async-start | bytes 113344512
  7.2 18.3 %slice-start.6 = ((s8[16777216]{0:T(1024)(128)(4,1)}), s8[4194304]{0:T(1024)(128)(4,1)S(1)}, s32[]{:S(2)}) async-start(s8[16777216]{0:T(1024)(128)(4,1)} %bitcast.25), calls=%async_computation.8 | async-start | bytes 8388608
  7.2 18.3 %slice-start.7 = ((s8[16777216]{0:T(1024)(128)(4,1)}), s8[4194304]{0:T(1024)(128)(4,1)S(1)}, s32[]{:S(2)}) async-start(s8[16777216]{0:T(1024)(128)(4,1)} %bitcast.25), calls=%async_computation.9 | async-start | bytes 8388608
  17.4 8.1 slice-start.8
  17.4 8.5 slice-start.9
  45.6 24.9 %slice-start.3 = ((s8[11534336]{0:T(1024)(128)(4,1)}), s8[4194304]{0:T(1024)(128)(4,1)S(1)}, s32[]{:S(2)}) async-start(s8[11534336]{0:T(1024)(128)(4,1)} %bitcast.22), calls=%async_computation.5 | async-start | bytes 8388608
  45.6 24.9 %slice-start.4 = ((s8[11534336]{0:T(1024)(128)(4,1)}), s8[3145728]{0:T(1024)(128)(4,1)S(1)}, s32[]{:S(2)}) async-start(s8[11534336]{0:T(1024)(128)(4,1)} %bitcast.22), calls=%async_computation.6 | async-start | bytes 6291456
  57.4 13.2 %slice-start.5 = ((s8[11534336]{0:T(1024)(128)(4,1)}), s8[4194304]{0:T(1024)(128)(4,1)S(1)}, s32[]{:S(2)}) async-start(s8[11534336]{0:T(1024)(128)(4,1)} %bitcast.22), calls=%async_computation.7 | async-start | bytes 8388608
  57.4 19.1 %slice-start = ((s8[11534336]{0:T(1024)(128)(4,1)}), s8[4194304]{0:T(1024)(128)(4,1)S(1)}, s32[]{:S(2)}) async-start(s8[11534336]{0:T(1024)(128)(4,1)} %bitcast.19), calls=%async_computation.2 | async-start | bytes 8388608
  57.4 19.1 %slice-start.1 = ((s8[11534336]{0:T(1024)(128)(4,1)}), s8[3145728]{0:T(1024)(128)(4,1)S(1)}, s32[]{:S(2)}) async-start(s8[11534336]{0:T(1024)(128)(4,1)} %bitcast.19), calls=%async_computation.3 | async-start | bytes 6291456
  70.6 7.2 slice-start.2
  77.8 4.5 copy-start.1
  83.0 827.9 %all-reduce.5.cloned.1.call-start = ((), (), s32[]{:S(2)}) async-start(), calls=%async_computation | async-start | bytes 56672256
  980.3 0.6 copy-start
Sparse Core Ops, SparseCore 0:
  83.1 507.1 all-reduce.6
  636.5 274.4 all-reduce.4
where the time goes:
time: 1050 us; the launch traced here: 1040 us
  waiting for transfers between devices  782 us (74%)
  local copies, waits for them, and re-layouts  238 us (23%)
  between operations  14.2 us (1%)
    unnamed x4, waiting for transfers between devices  782 us
    unnamed x43, local copies, waits for them, and re-layouts  108 us
    reshape x5, local copies, waits for them, and re-layouts, split_tensors(): pieces.append(flat_values[offset:offset + count].reshape(shape))  48.4 us
    broadcast_in_dim x1, local copies, waits for them, and re-layouts, own_chip_block(): return jnp.concatenate(block_list)[None, :]  41.2 us
    slice x3, local copies, waits for them, and re-layouts, split_tensors(): pieces.append(flat_values[offset:offset + count].reshape(shape))  21.7 us
  transfers between devices with their start and end apart: 2, of which 2 were waited for; matrix products, arithmetic and copies ran while one was open for 0% of the time, Pallas kernels for 0%

commit v1 on v0

v1 whole, which is shorter than its diff:
```python
import functools
import math
import jax
import jax.numpy as jnp
from jax import lax
from jax.experimental import pallas as pl
from jax.experimental.pallas import tpu as pltpu
from jax.sharding import PartitionSpec as P

MESH_AXES = ('outer', 'middle', 'inner')
MESH = pl.DeviceIdType.MESH
ADAM_BETA1 = 0.9
ADAM_BETA2 = 0.98
ADAM_EPS = 1e-9
LEARN_RATE = 0.05
ADAM_STEP = 3

LANES = 128
SLICE = 885488
TENSORS = ((0, 32768, 8), (32768, 65536, 32), (65536, 88064, 22), (88064, 110592, 8), (110592, 110720, 1))
ROWS = 110720
UNIT = 128
WINDOW = 7296
THIRD = WINDOW // 3
ITEMS = THIRD // UNIT
EDGE = 32768
OWN = 7200
OWN_THIRD = OWN // 3
OWN_CHUNK = 160
OWN_ITEMS = OWN_THIRD // OWN_CHUNK
SIXTEEN = 16


def floor_block(row):
    result = row
    for base, end, tiles in TENSORS:
        block = 8 * tiles if tiles > 1 else UNIT
        floored = base + (row - base) // block * block
        result = jnp.where((row >= base) & (row < end), floored, result)
    return result


def window_start(index):
    row = floor_block(index * (SLICE // 16) // 8)
    return jnp.minimum(row // UNIT * UNIT, ROWS - WINDOW)


def own_start_static(index):
    row = -(-index * SLICE // LANES)
    for base, end, tiles in TENSORS:
        if base <= row < end:
            block = 8 * tiles if tiles > 1 else UNIT
            return base + -(-(row - base) // block) * block
    return ROWS


OWN_STARTS = [own_start_static(d) for d in range(SIXTEEN)] + [ROWS]


def own_start(index):
    result = jnp.int32(0)
    for d in range(SIXTEEN):
        result = jnp.where(index == d, OWN_STARTS[d], result)
    return result


def adam_update(grad_mean, m_old, v_old, w_old):
    m_new = ADAM_BETA1 * m_old + (1.0 - ADAM_BETA1) * grad_mean
    v_new = ADAM_BETA2 * v_old + (1.0 - ADAM_BETA2) * (grad_mean * grad_mean)
    m_hat = m_new / (1.0 - ADAM_BETA1 ** ADAM_STEP)
    v_hat = v_new / (1.0 - ADAM_BETA2 ** ADAM_STEP)
    w_new = w_old - LEARN_RATE * m_hat / (jnp.sqrt(v_hat) + ADAM_EPS)
    return m_new, v_new, w_new


def to_tiles(tensor):
    rows, width = tensor.shape
    return tensor.reshape(rows // 8, 8, width // LANES, LANES).transpose(0, 2, 1, 3).reshape(-1, LANES)


def from_tiles(tiles, width):
    return tiles.reshape(-1, width // LANES, 8, LANES).transpose(0, 2, 1, 3).reshape(-1, width)


ORDERS = ((0, 1, 2), (1, 2, 0), (2, 0, 1))


def position():
    outer, middle, inner = (lax.axis_index(name) for name in MESH_AXES)
    return outer, middle, inner // 2, inner % 2


def neighbour(axis):
    outer, middle, x, core = position()
    z, y = outer, middle
    if axis == 0:
        z = 1 - z
    elif axis == 1:
        y = 1 - y
    elif axis == 2:
        x = 1 - x
    else:
        core = 1 - core
    return (z, y, 2 * x + core)


def scatter_kernel(e_ref, a_ref, f_ref, h_ref, b_ref, m_ref, v_ref, w_ref, out_ref, edge_ref,
                   part, recv0, recv1, recv2, mine, pair_send, pair_recv, mine_sem,
                   send0, send1, send2, arrive0, arrive1, arrive2, out_sem, edge_send, edge_recv):
    z, y, x, core = position()
    chip = (z * 2 + y) * 2 + x
    device = chip * 2 + core
    sources = (e_ref, a_ref, f_ref, h_ref, b_ref)

    before = (device + SIXTEEN - 1) % SIXTEEN
    for n, ref in enumerate((m_ref, v_ref, w_ref)):
        pltpu.make_async_remote_copy(
            src_ref=ref.at[pl.ds(0, EDGE)], dst_ref=edge_ref.at[pl.ds(n * EDGE, EDGE)],
            send_sem=edge_send.at[n], recv_sem=edge_recv.at[n],
            device_id=(before // 8, before // 4 % 2, before % 4), device_id_type=MESH).start()

    def from_source(row, action):
        for source, (base, end, _) in zip(sources, TENSORS):
            @pl.when((row >= base) & (row < end))
            def _():
                action(source.at[pl.ds(pl.multiple_of(row - base, UNIT), UNIT), :])

    def item_row(third, item):
        return pl.multiple_of(third * THIRD + item * UNIT, UNIT)

    def start_pair(item):
        @pl.loop(0, 8)
        def _(j):
            jz, jy, jx = j // 4, j // 2 % 2, j % 2
            other = ((z + jz) % 2 * 2 + (y + jy) % 2) * 2 + (x + jx) % 2
            start = window_start(other * 2 + 1 - core)
            for third in range(3):
                row = item_row(third, item)
                from_source(start + row, lambda src: pltpu.make_async_remote_copy(
                    src_ref=src, dst_ref=part.at[jz, jy, jx, pl.ds(row, UNIT), :],
                    send_sem=pair_send.at[third, item], recv_sem=pair_recv.at[third, item],
                    device_id=neighbour(3), device_id_type=MESH).start())

    def start_mine(item, slot):
        @pl.loop(0, 8)
        def _(j):
            jz, jy, jx = j // 4, j // 2 % 2, j % 2
            other = ((z + jz) % 2 * 2 + (y + jy) % 2) * 2 + (x + jx) % 2
            start = window_start(other * 2 + core)
            for third in range(3):
                row = item_row(third, item)
                from_source(start + row, lambda src: pltpu.make_async_copy(
                    src, mine.at[slot, third, jz, jy, jx], mine_sem.at[slot]).start())

    def hop_copy(third, item, hop):
        rows = pl.ds(item_row(third, item), UNIT)
        first, second, last = ORDERS[third]
        if hop == 0:
            index = tuple(1 if n == first else slice(None) for n in range(3))
            target = recv0.at[:, :, rows, :]
        elif hop == 1:
            index = tuple(0 if n == first else 1 if n == second else slice(None) for n in range(3))
            target = recv1.at[:, rows, :]
        else:
            index = tuple(1 if n == last else 0 for n in range(3))
            target = recv2.at[rows, :]
        return pltpu.make_async_remote_copy(
            src_ref=part.at[index + (rows, slice(None))], dst_ref=target,
            send_sem=(send0, send1, send2)[hop].at[third, item], recv_sem=(arrive0, arrive1, arrive2)[hop].at[third, item],
            device_id=neighbour(ORDERS[third][hop]), device_id_type=MESH)

    def pair_all(third, item):
        block = part.at[:, :, :, pl.ds(item_row(third, item), UNIT), :]
        return pltpu.make_async_remote_copy(
            src_ref=block, dst_ref=block, send_sem=pair_send.at[third, item], recv_sem=pair_recv.at[third, item],
            device_id=neighbour(3), device_id_type=MESH)

    def out_copy(third, item):
        rows = pl.ds(item_row(third, item), UNIT)
        return pltpu.make_async_copy(part.at[0, 0, 0, rows, :], out_ref.at[rows, :], out_sem.at[third, item])

    start_mine(0, 0)
    start_pair(0)
    start_pair(1)

    @pl.loop(0, ITEMS + 4)
    def _(step):
        @pl.when(step < ITEMS)
        def _():
            slot = step % 2

            @pl.when(step + 1 < ITEMS)
            def _():
                start_mine(step + 1, 1 - slot)

            @pl.when(step + 2 < ITEMS)
            def _():
                start_pair(step + 2)

            pltpu.make_async_copy(mine.at[slot], mine.at[slot], mine_sem.at[slot]).wait()
            for third in range(3):
                rows = pl.ds(item_row(third, step), UNIT)
                pair_all(third, step).wait_recv()
                for j in range(8):
                    index = (j // 4, j // 2 % 2, j % 2)
                    part[index + (rows, slice(None))] += mine[(slot, third) + index]
                hop_copy(third, step, 0).start()

        @pl.when((step >= 1) & (step < ITEMS + 1))
        def _():
            item = step - 1
            for third in range(3):
                rows = pl.ds(item_row(third, item), UNIT)
                hop_copy(third, item, 0).wait_recv()
                first = ORDERS[third][0]
                for j in range(4):
                    pair = [j // 2, j % 2]
                    index = tuple(pair[:first] + [0] + pair[first:])
                    part[index + (rows, slice(None))] += recv0[j // 2, j % 2, rows, :]
                hop_copy(third, item, 1).start()

        @pl.when((step >= 2) & (step < ITEMS + 2))
        def _():
            item = step - 2
            for third in range(3):
                rows = pl.ds(item_row(third, item), UNIT)
                hop_copy(third, item, 1).wait_recv()
                last = ORDERS[third][2]
                for j in range(2):
                    index = tuple(j if n == last else 0 for n in range(3))
                    part[index + (rows, slice(None))] += recv1[j, rows, :]
                hop_copy(third, item, 2).start()

        @pl.when((step >= 3) & (step < ITEMS + 3))
        def _():
            item = step - 3
            for third in range(3):
                rows = pl.ds(item_row(third, item), UNIT)
                hop_copy(third, item, 2).wait_recv()
                part[0, 0, 0, rows, :] = (part[0, 0, 0, rows, :] + recv2[rows, :]) / SIXTEEN

        @pl.when(step >= 4)
        def _():
            for third in range(3):
                out_copy(third, step - 4).start()

    @pl.loop(0, ITEMS)
    def _(item):
        for third in range(3):
            pair_all(third, item).wait_send()
            for hop in range(3):
                hop_copy(third, item, hop).wait_send()
            out_copy(third, item).wait()

    for n, ref in enumerate((m_ref, v_ref, w_ref)):
        pltpu.make_async_remote_copy(
            src_ref=ref.at[pl.ds(0, EDGE)], dst_ref=edge_ref.at[pl.ds(n * EDGE, EDGE)],
            send_sem=edge_send.at[n], recv_sem=edge_recv.at[n],
            device_id=(before // 8, before // 4 % 2, before % 4), device_id_type=MESH).wait()


def scatter(grads, m, v, w):
    any_spec = pl.BlockSpec(memory_space=pl.ANY)
    dma = pltpu.SemaphoreType.DMA
    return pl.pallas_call(
        scatter_kernel,
        out_shape=(jax.ShapeDtypeStruct((WINDOW, LANES), jnp.float32), jax.ShapeDtypeStruct((3 * EDGE,), jnp.float32)),
        in_specs=[any_spec] * 8,
        out_specs=(any_spec, any_spec),
        scratch_shapes=[
            pltpu.VMEM((2, 2, 2, WINDOW, LANES), jnp.float32),
            pltpu.VMEM((2, 2, WINDOW, LANES), jnp.float32),
            pltpu.VMEM((2, WINDOW, LANES), jnp.float32),
            pltpu.VMEM((WINDOW, LANES), jnp.float32),
            pltpu.VMEM((2, 3, 2, 2, 2, UNIT, LANES), jnp.float32),
            dma((3, ITEMS)), dma((3, ITEMS)), dma((2,)),
            dma((3, ITEMS)), dma((3, ITEMS)), dma((3, ITEMS)),
            dma((3, ITEMS)), dma((3, ITEMS)), dma((3, ITEMS)),
            dma((3, ITEMS)), dma((3,)), dma((3,)),
        ],
        compiler_params=pltpu.CompilerParams(has_side_effects=True, vmem_limit_bytes=67043328),
    )(*grads, m, v, w)


def gather_kernel(w_ref, full_ref, pair_send, pair_recv, send, arrive, own_sem):
    z, y, x, core = position()
    here = (z, y, x)

    def rows_of(third, item):
        return pl.ds(pl.multiple_of(third * OWN_THIRD + item * OWN_CHUNK, OWN_CHUNK), OWN_CHUNK)

    own = pltpu.make_async_copy(w_ref, full_ref.at[z, y, x, core], own_sem)
    own.start()

    def copy(third, item, hop):
        rows = rows_of(third, item)
        order = ORDERS[third]
        if hop == 0:
            source = w_ref.at[rows, :]
            target = full_ref.at[z, y, x, core, rows, :]
        else:
            index = tuple(slice(None) if n in order[:hop] else here[n] for n in range(3))
            source = target = full_ref.at[index + (core, rows, slice(None))]
        return pltpu.make_async_remote_copy(
            src_ref=source, dst_ref=target, send_sem=send.at[third, item, hop], recv_sem=arrive.at[third, item, hop],
            device_id=neighbour(order[hop]), device_id_type=MESH)

    def arrival(third, item, hop):
        rows = rows_of(third, item)
        order = ORDERS[third]
        index = tuple(slice(None) if n in order[:hop] else (1 - here[n] if n == order[hop] else here[n]) for n in range(3))
        block = full_ref.at[index + (core, rows, slice(None))]
        return pltpu.make_async_remote_copy(
            src_ref=block, dst_ref=block, send_sem=send.at[third, item, hop], recv_sem=arrive.at[third, item, hop],
            device_id=neighbour(order[hop]), device_id_type=MESH)

    def pair(third, item, side):
        block = full_ref.at[:, :, :, side, rows_of(third, item), :]
        return pltpu.make_async_remote_copy(
            src_ref=block, dst_ref=block, send_sem=pair_send.at[third, item], recv_sem=pair_recv.at[third, item],
            device_id=neighbour(3), device_id_type=MESH)

    for third in range(3):
        copy(third, 0, 0).start()
    own.wait()

    @pl.loop(0, OWN_ITEMS + 3)
    def _(step):
        @pl.when(step + 1 < OWN_ITEMS)
        def _():
            for third in range(3):
                copy(third, step + 1, 0).start()

        for hop in range(1, 4):
            @pl.when((step >= hop - 1) & (step < OWN_ITEMS + hop - 1))
            def _():
                item = step - (hop - 1)
                for third in range(3):
                    arrival(third, item, hop - 1).wait_recv()
                    if hop < 3:
                        copy(third, item, hop).start()
                    else:
                        pair(third, item, core).start()

    @pl.loop(0, OWN_ITEMS)
    def _(item):
        for third in range(3):
            pair(third, item, 1 - core).wait_recv()
            pair(third, item, core).wait_send()
            for hop in range(3):
                copy(third, item, hop).wait_send()


def gather(w_own):
    dma = pltpu.SemaphoreType.DMA
    return pl.pallas_call(
        gather_kernel,
        out_shape=jax.ShapeDtypeStruct((2, 2, 2, 2, OWN, LANES), jnp.bfloat16),
        in_specs=[pl.BlockSpec(memory_space=pltpu.VMEM)],
        out_specs=pl.BlockSpec(memory_space=pl.ANY),
        scratch_shapes=[
            dma((3, OWN_ITEMS)), dma((3, OWN_ITEMS)), dma((3, OWN_ITEMS, 3)), dma((3, OWN_ITEMS, 3)), dma(()),
        ],
        compiler_params=pltpu.CompilerParams(has_side_effects=True),
    )(w_own)


def device_index():
    outer, middle, inner = (lax.axis_index(name) for name in MESH_AXES)
    return (outer * 2 + middle) * 4 + inner


def for_blocks(start, length, action):
    for base, end, tiles in TENSORS:
        block = 8 * tiles
        low = (jnp.maximum(start, base) - base + block - 1) // block
        high = jnp.maximum(jnp.minimum(start + length, end) - base, 0) // block

        @pl.loop(low, jnp.maximum(high, low))
        def _(n):
            action(pl.multiple_of(base + n * block - start, 8), tiles)


def flat_kernel(tile_ref, flat_ref):
    def action(row, tiles):
        for t in range(tiles):
            flat_ref[pl.ds(row + t, 8, stride=tiles), :] = tile_ref[pl.ds(row + 8 * t, 8), :]
    for_blocks(window_start(device_index()), WINDOW, action)


def tile_kernel(flat_ref, tile_ref, work):
    def action(row, tiles):
        for t in range(tiles):
            work[pl.ds(row + 8 * t, 8), :] = flat_ref[pl.ds(row + t, 8, stride=tiles), :]
    for_blocks(own_start(device_index()), OWN, action)
    tile_ref[...] = work[...].astype(jnp.bfloat16)


def chip_kernel(e_ref, a_ref, f_ref, h_ref, b_ref, out_ref, buf, sems):
    chip = device_index() // 2
    offset = 0
    copies = []
    for n, ref in enumerate((e_ref, a_ref, f_ref, h_ref)):
        base, end, tiles = TENSORS[n]
        rows = (end - base) // 8
        copies.append((pltpu.make_async_copy(
            ref.at[pl.ds(pl.multiple_of(chip * rows, rows), rows), :], buf.at[pl.ds(offset, rows), :], sems.at[n]),
            offset, rows, tiles))
        copies[-1][0].start()
        offset += rows
    out_ref[pl.ds(offset, 16), :] = b_ref[...]
    for copy, first, rows, tiles in copies:
        copy.wait()

        @pl.loop(0, rows // (16 * tiles))
        def _(n):
            for half in range(2):
                row = pl.multiple_of(first + n * 16 * tiles + half * 8 * tiles, 16) if tiles % 2 == 0 else None
                for t in range(0, tiles, 2):
                    value = buf[pl.ds(row + 8 * t, 16), :].astype(jnp.float32)
                    out_ref[pl.ds(row + t, 8, stride=tiles), :] = value[:8]
                    out_ref[pl.ds(row + t + 1, 8, stride=tiles), :] = value[8:]


CHIP_ROWS = 13824 + 16


def solution(mesh):
    vmem = pl.BlockSpec(memory_space=pltpu.VMEM)
    any_spec = pl.BlockSpec(memory_space=pl.ANY)

    def local_step(g_embed, g_attn, g_ffn_in, g_ffn_out, g_vec, m_shard, v_shard, w_shard):
        device = device_index()
        vec_count = g_vec.size
        grads = [to_tiles(g[0] if g.ndim == 3 else g[0, 0]) for g in (g_embed, g_attn, g_ffn_in, g_ffn_out)]
        grads.append(jnp.pad(g_vec.reshape(-1), (0, UNIT * LANES - vec_count)).reshape(UNIT, LANES))
        mean_tiles, edges = scatter(grads, m_shard, v_shard, w_shard)

        mean_flat = pl.pallas_call(
            flat_kernel, out_shape=jax.ShapeDtypeStruct((WINDOW + 512, LANES), jnp.float32),
            in_specs=[vmem], out_specs=vmem)(mean_tiles).reshape(-1)
        start = window_start(device) * LANES
        mean_ext = lax.dynamic_slice(mean_flat, (device * SLICE - start,), (SLICE + EDGE,))
        m_new, v_new, w_new = adam_update(mean_ext[:SLICE], m_shard, v_shard, w_shard)
        w_edge = adam_update(mean_ext[SLICE:], edges[:EDGE], edges[EDGE:2 * EDGE], edges[2 * EDGE:])[2]
        w_ext = jnp.concatenate([w_new, w_edge, jnp.zeros(((OWN + 512) * LANES - SLICE - EDGE,), jnp.float32)])
        w_rows = lax.dynamic_slice(w_ext, (own_start(device) * LANES - device * SLICE,), (OWN * LANES,)).reshape(OWN, LANES)
        w_own = pl.pallas_call(
            tile_kernel, out_shape=jax.ShapeDtypeStruct((OWN, LANES), jnp.bfloat16),
            in_specs=[vmem], out_specs=vmem, scratch_shapes=[pltpu.VMEM((OWN, LANES), jnp.float32)])(w_rows)

        full = gather(w_own).reshape(SIXTEEN, OWN, LANES)
        tiles = []
        for base, end, _ in TENSORS:
            pieces = []
            for d in range(SIXTEEN):
                low, high = max(OWN_STARTS[d], base), min(OWN_STARTS[d + 1], end)
                if low < high:
                    pieces.append(full[d, low - OWN_STARTS[d]:high - OWN_STARTS[d]])
            tiles.append(jnp.concatenate(pieces, axis=0))
        vec = tiles[4].reshape(-1)[:vec_count]
        tensors = [from_tiles(t, g.shape[-1]).reshape(g.shape[1:]) for t, g in zip(tiles[:4], (g_embed, g_attn, g_ffn_in, g_ffn_out))]

        block = vec_count // 8
        vec_block = lax.dynamic_slice(vec.astype(jnp.float32), (device // 2 * block,), (block,))
        vec_block = jnp.pad(vec_block, (0, 16 * LANES - block)).reshape(16, LANES)
        chip = pl.pallas_call(
            chip_kernel, out_shape=jax.ShapeDtypeStruct((CHIP_ROWS, LANES), jnp.float32),
            in_specs=[any_spec] * 4 + [vmem], out_specs=vmem,
            scratch_shapes=[pltpu.VMEM((13824, LANES), jnp.bfloat16), pltpu.SemaphoreType.DMA((4,))])(*tiles[:4], vec_block)
        w_chip = chip.reshape(1, -1)[:, :13824 * LANES + block].astype(jnp.bfloat16)
        return (m_new, v_new, w_new) + tuple(tensors) + (vec[None], w_chip)

    return jax.shard_map(local_step, mesh=mesh, in_specs=(P(MESH_AXES),) * 8, out_specs=(P(MESH_AXES),) * 3 + (P(),) * 5 + (P(MESH_AXES),), check_vma=False)
```

time: 1050 us -> 556 us (0.53)
  waiting for transfers between devices: 782 us -> 0 us
  Pallas kernels: 0 us -> 331 us
  local copies, waits for them, and re-layouts: 238 us -> 128 us
  other arithmetic: 9.04 us -> 94.6 us
  between operations: 14.2 us -> 0.78 us
    unnamed x4 -> x0, waiting for transfers between devices: 782 us -> none
    pallas_call x0 -> x5, Pallas kernels: none -> 331 us  [the longest x1 207 us: scatter(): pl.pallas_call(scatter_kernel, out_shape=(jax.ShapeDtypeStruct((WINDOW, L...]
    concatenate x0 -> x1, other arithmetic: none -> 76.7 us  [local_step(): tiles.append(jnp.concatenate(pieces, axis=0))]
    reshape x7 -> x3, local copies, waits for them, and re-layouts: 63.7 us -> 6.14 us  [the longest x1 4.9 us: local_step(): lax.dynamic_slice(w_ext, (own_start(device) * LANES - device * SLICE,), (...]
    broadcast_in_dim x1, local copies, waits for them, and re-layouts: 41.2 us -> 0.73 us  [local_step(): jnp.zeros(((OWN + 512) * LANES - SLICE - EDGE,), jnp.float32)]
    unnamed x43 -> x15, local copies, waits for them, and re-layouts: 108 us -> 71.6 us
    concatenate x2 -> x3, local copies, waits for them, and re-layouts: 1.41 us -> 28.5 us  [the longest x1 25.3 us: local_step(): jnp.concatenate([w_new, w_edge, jnp.zeros(((OWN + 512) * LANES - SLICE -...]
    sub x0 -> x2, other arithmetic: none -> 13.6 us  [adam_update(): w_new = w_old - LEARN_RATE * m_hat / (jnp.sqrt(v_hat) + ADAM_EPS)]
  transfers between devices with their start and end apart: 2 -> 0, of which waited for: 2 -> 0; matrix products, arithmetic and copies ran while one was open for 0% -> 0% of each run, Pallas kernels for 0% -> 0%
where the time goes in v1:
time: 556 us; the launch traced here: 555 us
  Pallas kernels  331 us (60%)
  local copies, waits for them, and re-layouts  128 us (23%)
  other arithmetic  94.6 us (17%)
    pallas_call x1, Pallas kernels, scatter(): pl.pallas_call(scatter_kernel, out_shape=(jax.ShapeDtypeStruct((WINDOW, L...  207 us
    pallas_call x1, Pallas kernels, gather(): pl.pallas_call(gather_kernel, out_shape=jax.ShapeDtypeStruct((2, 2, 2, 2,...  107 us
    concatenate x1, other arithmetic, local_step(): tiles.append(jnp.concatenate(pieces, axis=0))  76.7 us
    unnamed x15, local copies, waits for them, and re-layouts  71.6 us
    concatenate x1, local copies, waits for them, and re-layouts, local_step(): jnp.concatenate([w_new, w_edge, jnp.zeros(((OWN + 512) * LANES - SLICE -...  25.3 us
    sub x2, other arithmetic, adam_update(): w_new = w_old - LEARN_RATE * m_hat / (jnp.sqrt(v_hat) + ADAM_EPS)  13.6 us
    squeeze x7, local copies, waits for them, and re-layouts, local_step(): pieces.append(full[d, low - OWN_STARTS[d]:high - OWN_STARTS[d]])  12.9 us

profile of v1, /device:TPU:0, one launch (start us, length us, event | category | flops | bytes accessed | tf_op | source)
XLA Modules:
  0.0 555.1 jit_solution(15348467358592662855)
XLA Ops:
  0.6 0.9 reduce
  1.6 0.6 pad_bitcast_fusion.b_ref
  2.2 206.8 %shard_map.151 = (f32[7296,128]{1,0:T(8,128)}, f32[98304]{0:T(1024)}) custom-call(f32[32768,128]{1,0:T(8,128)} %bitcast.141, f32[32768,128]{1,0:T(8,128)} %bitcast.142, f32[22528,128]{1,0:T(8,128)} %bitcast.146, f32[22528,128]{1,0:T(8,128)} %bitcast.147, f32[128,128]{1,0:T(8,128)} %pad_bitcast_fusion.b_ref, f32[885488]{0:T(1024)} %m_ref.1, f32[885488]{0:T(1024)} %v_ref.1, ...), custom_call_target="tpu_custom_call" | custom-call | tf_op jit(solution)/shard_map/pallas_call | solution.py:265
  209.0 5.3 shard_map.152
  214.3 11.0 %divide_subtract_fusion = (f32[885488]{0:T(1024)S(1)}, f32[885488]{0:T(1024)}, f32[885488]{0:T(1024)}) fusion(f32[885488]{0:T(1024)} %w_ref.1, f32[999424]{0:T(1024)} %bitcast.143, s32[]{:T(128)S(6)} %select_n.109, f32[885488]{0:T(1024)} %v_ref.1, f32[885488]{0:T(1024)} %m_ref.1), kind=kLoop, calls=%fused_computation.5 | loop fusion | flops 10625856 | bytes 24793668 | tf_op jit(solution)/shard_map/sub | solution.py:72
  225.3 0.0 copy-start
  225.3 2.5 divide_subtract_fusion.1
  227.9 0.7 broadcast_in_dim.6
  228.6 25.3 %concatenate.15 = f32[987136]{0:T(1024)} concatenate(f32[885488]{0:T(1024)S(1)} %get-tuple-element.13, f32[32768]{0:T(1024)} %divide_subtract_fusion.1, f32[68880]{0:T(1024)} %broadcast_in_dim.6), dimensions={0} | concatenate | bytes 7897088 | tf_op jit(solution)/shard_map/concatenate | solution.py:446
  253.8 4.9 dynamic-slice_bitcast_fusion.flat_ref
  258.7 0.0 copy-done
  258.7 4.5 shard_map.153.w_ref
  263.3 107.2 %shard_map.154 = bf16[2,2,2,2,7200,128]{5,4,3,2,1,0:T(8,128)(2,1)} custom-call(bf16[7200,128]{1,0:T(8,128)(2,1)} %shard_map.153.w_ref), custom_call_target="tpu_custom_call" | custom-call | tf_op jit(solution)/shard_map/pallas_call | solution.py:356
  370.5 1.1 fusion.10
  371.6 1.7 fusion.4
  373.3 1.6 fusion
  374.9 2.5 fusion.3
  377.4 2.5 fusion.2
  379.8 2.5 fusion.1
  382.3 1.5 fusion.8.e_ref
  383.8 0.0 copy-start.1
  383.8 1.8 fusion.9.a_ref
  385.6 0.0 copy-start.2
  385.6 2.3 slice_bitcast_fusion.14
  388.0 2.8 slice_bitcast_fusion.11
  390.8 1.6 slice_bitcast_fusion
  392.4 1.3 slice_bitcast_fusion.15
  393.6 0.0 copy-done.1
  393.7 1.6 slice_bitcast_fusion.12
  395.2 0.0 copy-done.2
  395.2 2.2 slice_bitcast_fusion.3
  397.5 1.1 slice_bitcast_fusion.18
  398.6 76.7 %pad_maximum_fusion = (bf16[22528,128]{1,0:T(8,128)(2,1)}, bf16[22528,128]{1,0:T(8,128)(2,1)}) fusion(bf16[4928,128]{1,0:T(8,128)(2,1)S(1)} %slice_bitcast_fusion.14, bf16[6864,128]{1,0:T(8,128)(2,1)S(1)} %slice_bitcast_fusion.11, bf16[7040,128]{1,0:T(8,128)(2,1)S(1)} %slice_bitcast_fusion, bf16[3696,128]{1,0:T(8,128)(2,1)S(1)} %slice_bitcast_fusion.15, ...), kind=kLoop, calls=%fused_computation.1 | loop fusion | flops 46137344 | bytes 23068672 | tf_op jit(solution)/shard_map/concatenate | solution.py:460
  475.3 0.7 slice_bitcast_fusion.19
  476.0 0.7 copy.22
  476.7 0.1 dynamic-slice_convert_fusion
  476.8 0.6 pad_bitcast_fusion.1.b_ref
  477.4 7.4 %shard_map.155 = f32[13840,128]{1,0:T(8,128)} custom-call(bf16[32768,128]{1,0:T(8,128)(2,1)} %copy-done.1, bf16[32768,128]{1,0:T(8,128)(2,1)} %copy-done.2, bf16[22528,128]{1,0:T(8,128)(2,1)} %get-tuple-element.26.f_ref, bf16[22528,128]{1,0:T(8,128)(2,1)} %get-tuple-element.27.h_ref, f32[16,128]{1,0:T(8,128)} %pad_bitcast_fusion.1.b_ref), custom_call_target="tpu_custom_call" | custom-call | tf_op jit(solution)/shard_map/pallas_call | solution.py:467
  484.8 3.3 convert_bitcast_fusion
  488.1 58.4 %copy.21 = bf16[1,1,13840,128]{3,1,2,0:T(2,128)(2,1)S(1)} copy(bf16[1,1,13840,128]{3,2,1,0:T(8,128)(2,1)S(1)} %convert_bitcast_fusion) | data formatting | bytes 7086080
  546.6 8.6 %slice.128 = bf16[1,1770976]{1,0:T(2,128)(2,1)} slice(bf16[1,1771520]{1,0:T(2,128)(2,1)S(1)} %bitcast.138), slice={[0:1], [0:1770976]} | slice | bytes 7083904 | tf_op jit(solution)/shard_map/slice | solution.py:471
Async XLA Ops:
  225.3 33.4 %copy-start = (f32[885488]{0:T(1024)}, f32[885488]{0:T(1024)S(1)}, u32[]{:S(2)}) copy-start(f32[885488]{0:T(1024)S(1)} %get-tuple-element.13) | copy-start | bytes 10625860
  383.8 9.9 %copy-start.1 = (bf16[32768,128]{1,0:T(8,128)(2,1)}, bf16[32768,128]{1,0:T(8,128)(2,1)S(1)}, u32[]{:S(2)}) copy-start(bf16[32768,128]{1,0:T(8,128)(2,1)S(1)} %fusion.8.e_ref) | copy-start | bytes 25165828
  385.6 9.6 %copy-start.2 = (bf16[32768,128]{1,0:T(8,128)(2,1)}, bf16[32768,128]{1,0:T(8,128)(2,1)S(1)}, u32[]{:S(2)}) copy-start(bf16[32768,128]{1,0:T(8,128)(2,1)S(1)} %fusion.9.a_ref) | copy-start | bytes 25165828

commit v2 on v1

--- a/solution.py
+++ b/solution.py
@@ -29,6 +29,8 @@
 OWN_CHUNK = 160
 OWN_ITEMS = OWN_THIRD // OWN_CHUNK
 SIXTEEN = 16
+FINAL_LIMIT = 20000000
+GATHER_LIMIT = 6000000
 
 
 def floor_block(row):
@@ -357,11 +359,11 @@
         gather_kernel,
         out_shape=jax.ShapeDtypeStruct((2, 2, 2, 2, OWN, LANES), jnp.bfloat16),
         in_specs=[pl.BlockSpec(memory_space=pltpu.VMEM)],
-        out_specs=pl.BlockSpec(memory_space=pl.ANY),
+        out_specs=pl.BlockSpec(memory_space=pltpu.VMEM),
         scratch_shapes=[
             dma((3, OWN_ITEMS)), dma((3, OWN_ITEMS)), dma((3, OWN_ITEMS, 3)), dma((3, OWN_ITEMS, 3)), dma(()),
         ],
-        compiler_params=pltpu.CompilerParams(has_side_effects=True),
+        compiler_params=pltpu.CompilerParams(has_side_effects=True, vmem_limit_bytes=GATHER_LIMIT),
     )(w_own)
 
 
@@ -381,94 +383,235 @@
             action(pl.multiple_of(base + n * block - start, 8), tiles)
 
 
-def flat_kernel(tile_ref, flat_ref):
-    def action(row, tiles):
+PAD = 8
+FLAT_ROWS = WINDOW + 272
+SHARD_VREGS = SLICE // 1024
+TAIL_ROWS = SLICE % 1024 // LANES
+TAIL_LANES = SLICE % LANES
+EDGE_ROWS = EDGE // LANES
+OWN_FLAT_ROWS = OWN + 512
+
+
+def lane_index():
+    return lax.broadcasted_iota(jnp.int32, (8, LANES), 1)
+
+
+def mid_kernel(tile_ref, m_ref, v_ref, w_ref, edge_ref, m_out, v_out, w_out, own_ref, flat, shifted, edged, aligned, tiled):
+    device = device_index()
+    start = window_start(device)
+
+    def to_flat(row, tiles):
         for t in range(tiles):
-            flat_ref[pl.ds(row + t, 8, stride=tiles), :] = tile_ref[pl.ds(row + 8 * t, 8), :]
-    for_blocks(window_start(device_index()), WINDOW, action)
-
-
-def tile_kernel(flat_ref, tile_ref, work):
-    def action(row, tiles):
+            flat[pl.ds(row + t, 8, stride=tiles), :] = tile_ref[pl.ds(row + 8 * t, 8), :]
+    for_blocks(start, WINDOW, to_flat)
+
+    first_row = device * (SLICE // 16) // 8
+    next_row = (device + 1) * (SLICE // 16) // 8
+    shift = device * SLICE - first_row * LANES
+    next_shift = (device + 1) * SLICE - next_row * LANES
+    lane = lane_index()
+
+    def mean_rows(row, amount):
+        here = flat[pl.ds(row, 8), :]
+        below = flat[pl.ds(row + 1, 8), :]
+        back = (LANES - amount) % LANES
+        return jnp.where(lane < LANES - amount, pltpu.roll(here, back, 1), pltpu.roll(below, back, 1))
+
+    def shard_step(n):
+        at = pl.ds(pl.multiple_of(n * 1024, 1024), 1024)
+        mean = mean_rows(first_row - start + n * 8, shift)
+        m_new, v_new, w_new = adam_update(mean, *(ref[at].reshape(8, LANES) for ref in (m_ref, v_ref, w_ref)))
+        m_out[at] = m_new.reshape(1024)
+        v_out[at] = v_new.reshape(1024)
+        w_out[at] = w_new.reshape(1024)
+        shifted[pl.ds(pl.multiple_of(PAD + n * 8, 8), 8), :] = pltpu.roll(w_new, shift, 1)
+
+    @pl.loop(0, SHARD_VREGS // 4)
+    def _(n):
+        for k in range(4):
+            shard_step(n * 4 + k)
+    for n in range(SHARD_VREGS // 4 * 4, SHARD_VREGS):
+        shard_step(n)
+
+    mean = mean_rows(first_row - start + SHARD_VREGS * 8, shift)
+    for r in range(TAIL_ROWS + 1):
+        size = LANES if r < TAIL_ROWS else TAIL_LANES
+        at = pl.ds(SHARD_VREGS * 1024 + r * LANES, size)
+        m_new, v_new, w_new = adam_update(
+            mean[r:r + 1, :size], *(ref[at].reshape(1, size) for ref in (m_ref, v_ref, w_ref)))
+        m_out[at] = m_new.reshape(size)
+        v_out[at] = v_new.reshape(size)
+        w_out[at] = w_new.reshape(size)
+        flat[pl.ds(FLAT_ROWS - 8 + r, 1), pl.ds(0, size)] = w_new
+    shifted[pl.ds(PAD + SHARD_VREGS * 8, 8), :] = pltpu.roll(flat[pl.ds(FLAT_ROWS - 8, 8), :], shift, 1)
+
+    @pl.loop(0, EDGE_ROWS // 8)
+    def _(n):
+        mean = mean_rows(next_row - start + n * 8, next_shift)
+        old = (edge_ref[pl.ds(pl.multiple_of(k * EDGE + n * 1024, 1024), 1024)].reshape(8, LANES) for k in range(3))
+        edged[pl.ds(pl.multiple_of(PAD + n * 8, 8), 8), :] = pltpu.roll(adam_update(mean, *old)[2], next_shift, 1)
+
+    own = own_start(device)
+    skip = own - first_row
+
+    @pl.loop(0, SHARD_VREGS + 1)
+    def _(n):
+        row = PAD + skip + n * 8
+        aligned[pl.ds(pl.multiple_of(n * 8, 8), 8), :] = jnp.where(
+            lane >= shift, shifted[pl.ds(row, 8), :], shifted[pl.ds(row - 1, 8), :])
+    edged[pl.ds(PAD - 1, 1), :] = aligned[pl.ds(next_row - own, 1), :]
+
+    @pl.loop(0, EDGE_ROWS // 8)
+    def _(n):
+        row = PAD + n * 8
+        aligned[pl.ds(next_row - own + n * 8, 8), :] = jnp.where(
+            lane >= next_shift, edged[pl.ds(row, 8), :], edged[pl.ds(row - 1, 8), :])
+
+    def to_tile(row, tiles):
         for t in range(tiles):
-            work[pl.ds(row + 8 * t, 8), :] = flat_ref[pl.ds(row + t, 8, stride=tiles), :]
-    for_blocks(own_start(device_index()), OWN, action)
-    tile_ref[...] = work[...].astype(jnp.bfloat16)
-
-
-def chip_kernel(e_ref, a_ref, f_ref, h_ref, b_ref, out_ref, buf, sems):
+            tiled[pl.ds(row + 8 * t, 8), :] = aligned[pl.ds(row + t, 8, stride=tiles), :]
+    for_blocks(own, OWN, to_tile)
+
+    @pl.loop(0, OWN // 32)
+    def _(n):
+        rows = pl.ds(pl.multiple_of(n * 32, 32), 32)
+        own_ref[rows, :] = tiled[rows, :].astype(jnp.bfloat16)
+
+
+def mid(mean_tiles, m, v, w, edges):
+    vmem = pl.BlockSpec(memory_space=pltpu.VMEM)
+    shard = jax.ShapeDtypeStruct((SLICE,), jnp.float32)
+    return pl.pallas_call(
+        mid_kernel,
+        out_shape=(shard, shard, shard, jax.ShapeDtypeStruct((OWN, LANES), jnp.bfloat16)),
+        in_specs=[vmem] * 5, out_specs=(vmem,) * 4,
+        scratch_shapes=[
+            pltpu.VMEM((FLAT_ROWS, LANES), jnp.float32),
+            pltpu.VMEM((PAD + SHARD_VREGS * 8 + 8 + 512, LANES), jnp.float32),
+            pltpu.VMEM((PAD + EDGE_ROWS, LANES), jnp.float32),
+            pltpu.VMEM((OWN_FLAT_ROWS, LANES), jnp.float32),
+            pltpu.VMEM((OWN, LANES), jnp.float32),
+        ],
+        compiler_params=pltpu.CompilerParams(vmem_limit_bytes=60000000),
+    )(mean_tiles, m, v, w, edges)
+
+
+def pieces_of(tensor):
+    base, end, _ = TENSORS[tensor]
+    for d in range(SIXTEEN):
+        low, high = max(OWN_STARTS[d], base), min(OWN_STARTS[d + 1], end)
+        if low < high:
+            yield d, low - OWN_STARTS[d], low - base, high - low
+
+
+PIECES = [(tensor,) + piece for tensor in range(4) for piece in pieces_of(tensor)]
+VEC_WIDTH = 12032
+VEC_ROWS = VEC_WIDTH // LANES
+VEC_BLOCK = VEC_WIDTH // 8
+CHIP_COUNTS = tuple((end - base) // 8 for base, end, _ in TENSORS[:4])
+CHIP_ROWS = sum(CHIP_COUNTS)
+CHIP_SIZE = CHIP_ROWS * LANES + VEC_BLOCK
+
+
+def final_kernel(full_ref, e_out, a_out, f_out, h_out, vec_out, chip_out, block, flat, vec, out_sem, block_sem):
+    outs = (e_out, a_out, f_out, h_out)
     chip = device_index() // 2
+    copies = []
+    for n, (tensor, d, source, target, rows) in enumerate(PIECES):
+        copies.append(pltpu.make_async_copy(
+            full_ref.at[d, pl.ds(source, rows), :], outs[tensor].at[pl.ds(target, rows), :], out_sem.at[n]))
+        copies[-1].start()
+
+    slot, source, _, _ = next(pieces_of(4))
+    vec[pl.ds(0, 96), :] = full_ref[slot, pl.ds(source, 96), :].astype(jnp.float32)
+    for n in range(VEC_ROWS // 8):
+        vec_out[:, n * 1024:(n + 1) * 1024] = vec[n * 8:n * 8 + 8, :].reshape(1, 1024).astype(jnp.bfloat16)
+    rest = VEC_ROWS % 8
+    vec_out[:, VEC_ROWS // 8 * 1024:] = vec[pl.ds(VEC_ROWS - rest, rest), :].reshape(1, rest * LANES).astype(jnp.bfloat16)
+
     offset = 0
-    copies = []
-    for n, ref in enumerate((e_ref, a_ref, f_ref, h_ref)):
-        base, end, tiles = TENSORS[n]
-        rows = (end - base) // 8
-        copies.append((pltpu.make_async_copy(
-            ref.at[pl.ds(pl.multiple_of(chip * rows, rows), rows), :], buf.at[pl.ds(offset, rows), :], sems.at[n]),
-            offset, rows, tiles))
-        copies[-1][0].start()
+    for tensor, rows in enumerate(CHIP_COUNTS):
+        base, _, tiles = TENSORS[tensor]
+        step = 16 * tiles
+
+        @pl.loop(0, rows // step)
+        def _(n):
+            row = base + chip * rows + n * step
+            slot = jnp.int32(0)
+            low = jnp.int32(0)
+            for d in range(1, SIXTEEN):
+                slot = jnp.where(row >= OWN_STARTS[d], d, slot)
+                low = jnp.where(row >= OWN_STARTS[d], OWN_STARTS[d], low)
+            second = row + 8 * tiles
+            slot2 = jnp.int32(0)
+            low2 = jnp.int32(0)
+            for d in range(1, SIXTEEN):
+                slot2 = jnp.where(second >= OWN_STARTS[d], d, slot2)
+                low2 = jnp.where(second >= OWN_STARTS[d], OWN_STARTS[d], low2)
+            for half, (at_slot, at_row) in enumerate(((slot, row - low), (slot2, second - low2))):
+                for t in range(0, tiles, 2):
+                    value = full_ref[at_slot, pl.ds(pl.multiple_of(at_row + 8 * t, 16), 16), :].astype(jnp.float32)
+                    for k in range(2):
+                        to = offset + n * step + half * 8 * tiles + t + k
+                        flat[pl.ds(to, 8, stride=tiles), :] = value[8 * k:8 * k + 8]
         offset += rows
-    out_ref[pl.ds(offset, 16), :] = b_ref[...]
-    for copy, first, rows, tiles in copies:
+
+    vec_row = chip * (VEC_BLOCK // 32) // 4
+    amount = chip * VEC_BLOCK - vec_row * LANES
+    back = (LANES - amount) % LANES
+    lane = lane_index()
+    for n in range(2):
+        here, below = vec[pl.ds(vec_row + n * 8, 8), :], vec[pl.ds(vec_row + n * 8 + 1, 8), :]
+        flat[pl.ds(CHIP_ROWS + n * 8, 8), :] = jnp.where(
+            lane < LANES - amount, pltpu.roll(here, back, 1), pltpu.roll(below, back, 1))
+
+    @pl.loop(0, CHIP_SIZE // 4096)
+    def _(n):
+        for k in range(4):
+            chip_out[:, pl.ds(pl.multiple_of(n * 4096 + k * 1024, 1024), 1024)] = flat[
+                pl.ds(pl.multiple_of(n * 32 + k * 8, 8), 8), :].reshape(1, 1024).astype(jnp.bfloat16)
+    for n in range(CHIP_SIZE // 4096 * 4, CHIP_SIZE // 1024):
+        chip_out[:, n * 1024:(n + 1) * 1024] = flat[n * 8:n * 8 + 8, :].reshape(1, 1024).astype(jnp.bfloat16)
+    done = CHIP_SIZE // 1024 * 1024
+    rows = (CHIP_SIZE - done) // LANES
+    last = CHIP_SIZE - done - rows * LANES
+    first = done // LANES
+    chip_out[:, done:done + rows * LANES] = flat[first:first + rows, :].reshape(1, rows * LANES).astype(jnp.bfloat16)
+    chip_out[:, CHIP_SIZE - last:] = flat[first + rows:first + rows + 1, :last].astype(jnp.bfloat16)
+
+    for copy in copies:
         copy.wait()
 
-        @pl.loop(0, rows // (16 * tiles))
-        def _(n):
-            for half in range(2):
-                row = pl.multiple_of(first + n * 16 * tiles + half * 8 * tiles, 16) if tiles % 2 == 0 else None
-                for t in range(0, tiles, 2):
-                    value = buf[pl.ds(row + 8 * t, 16), :].astype(jnp.float32)
-                    out_ref[pl.ds(row + t, 8, stride=tiles), :] = value[:8]
-                    out_ref[pl.ds(row + t + 1, 8, stride=tiles), :] = value[8:]
-
-
-CHIP_ROWS = 13824 + 16
-
-
-def solution(mesh):
+
+def finish(full):
     vmem = pl.BlockSpec(memory_space=pltpu.VMEM)
     any_spec = pl.BlockSpec(memory_space=pl.ANY)
-
+    shape = lambda rows: jax.ShapeDtypeStruct((rows, LANES), jnp.bfloat16)
+    return pl.pallas_call(
+        final_kernel,
+        out_shape=tuple(shape(end - base) for base, end, _ in TENSORS[:4]) + (
+            jax.ShapeDtypeStruct((1, VEC_WIDTH), jnp.bfloat16), jax.ShapeDtypeStruct((1, CHIP_SIZE), jnp.bfloat16)),
+        in_specs=[vmem], out_specs=(any_spec,) * 4 + (vmem, vmem),
+        scratch_shapes=[
+            pltpu.VMEM((16, LANES), jnp.bfloat16),
+            pltpu.VMEM((CHIP_ROWS + 16, LANES), jnp.float32),
+            pltpu.VMEM((120, LANES), jnp.float32),
+            pltpu.SemaphoreType.DMA((len(PIECES),)), pltpu.SemaphoreType.DMA(()),
+        ],
+        compiler_params=pltpu.CompilerParams(vmem_limit_bytes=FINAL_LIMIT),
+    )(full)
+
+
+def solution(mesh):
     def local_step(g_embed, g_attn, g_ffn_in, g_ffn_out, g_vec, m_shard, v_shard, w_shard):
-        device = device_index()
-        vec_count = g_vec.size
-        grads = [to_tiles(g[0] if g.ndim == 3 else g[0, 0]) for g in (g_embed, g_attn, g_ffn_in, g_ffn_out)]
-        grads.append(jnp.pad(g_vec.reshape(-1), (0, UNIT * LANES - vec_count)).reshape(UNIT, LANES))
+        matrices = (g_embed, g_attn, g_ffn_in, g_ffn_out)
+        grads = [to_tiles(g[0] if g.ndim == 3 else g[0, 0]) for g in matrices]
+        grads.append(jnp.pad(g_vec.reshape(-1), (0, UNIT * LANES - VEC_WIDTH)).reshape(UNIT, LANES))
         mean_tiles, edges = scatter(grads, m_shard, v_shard, w_shard)
-
-        mean_flat = pl.pallas_call(
-            flat_kernel, out_shape=jax.ShapeDtypeStruct((WINDOW + 512, LANES), jnp.float32),
-            in_specs=[vmem], out_specs=vmem)(mean_tiles).reshape(-1)
-        start = window_start(device) * LANES
-        mean_ext = lax.dynamic_slice(mean_flat, (device * SLICE - start,), (SLICE + EDGE,))
-        m_new, v_new, w_new = adam_update(mean_ext[:SLICE], m_shard, v_shard, w_shard)
-        w_edge = adam_update(mean_ext[SLICE:], edges[:EDGE], edges[EDGE:2 * EDGE], edges[2 * EDGE:])[2]
-        w_ext = jnp.concatenate([w_new, w_edge, jnp.zeros(((OWN + 512) * LANES - SLICE - EDGE,), jnp.float32)])
-        w_rows = lax.dynamic_slice(w_ext, (own_start(device) * LANES - device * SLICE,), (OWN * LANES,)).reshape(OWN, LANES)
-        w_own = pl.pallas_call(
-            tile_kernel, out_shape=jax.ShapeDtypeStruct((OWN, LANES), jnp.bfloat16),
-            in_specs=[vmem], out_specs=vmem, scratch_shapes=[pltpu.VMEM((OWN, LANES), jnp.float32)])(w_rows)
-
+        m_new, v_new, w_new, w_own = mid(mean_tiles, m_shard, v_shard, w_shard, edges)
         full = gather(w_own).reshape(SIXTEEN, OWN, LANES)
-        tiles = []
-        for base, end, _ in TENSORS:
-            pieces = []
-            for d in range(SIXTEEN):
-                low, high = max(OWN_STARTS[d], base), min(OWN_STARTS[d + 1], end)
-                if low < high:
-                    pieces.append(full[d, low - OWN_STARTS[d]:high - OWN_STARTS[d]])
-            tiles.append(jnp.concatenate(pieces, axis=0))
-        vec = tiles[4].reshape(-1)[:vec_count]
-        tensors = [from_tiles(t, g.shape[-1]).reshape(g.shape[1:]) for t, g in zip(tiles[:4], (g_embed, g_attn, g_ffn_in, g_ffn_out))]
-
-        block = vec_count // 8
-        vec_block = lax.dynamic_slice(vec.astype(jnp.float32), (device // 2 * block,), (block,))
-        vec_block = jnp.pad(vec_block, (0, 16 * LANES - block)).reshape(16, LANES)
-        chip = pl.pallas_call(
-            chip_kernel, out_shape=jax.ShapeDtypeStruct((CHIP_ROWS, LANES), jnp.float32),
-            in_specs=[any_spec] * 4 + [vmem], out_specs=vmem,
-            scratch_shapes=[pltpu.VMEM((13824, LANES), jnp.bfloat16), pltpu.SemaphoreType.DMA((4,))])(*tiles[:4], vec_block)
-        w_chip = chip.reshape(1, -1)[:, :13824 * LANES + block].astype(jnp.bfloat16)
-        return (m_new, v_new, w_new) + tuple(tensors) + (vec[None], w_chip)
+        *tiles, vec, w_chip = finish(full)
+        tensors = [from_tiles(t, g.shape[-1]).reshape(g.shape[1:]) for t, g in zip(tiles, matrices)]
+        return (m_new, v_new, w_new) + tuple(tensors) + (vec, w_chip)
 
     return jax.shard_map(local_step, mesh=mesh, in_specs=(P(MESH_AXES),) * 8, out_specs=(P(MESH_AXES),) * 3 + (P(),) * 5 + (P(MESH_AXES),), check_vma=False)

time: 556 us -> 395 us (0.71)
  local copies, waits for them, and re-layouts: 128 us -> 2.14 us
  other arithmetic: 94.6 us -> 0.91 us
  Pallas kernels: 331 us -> 391 us
    concatenate x1 -> x0, other arithmetic: 76.7 us -> none  [local_step(): tiles.append(jnp.concatenate(pieces, axis=0))]
    unnamed x15 -> x2, local copies, waits for them, and re-layouts: 71.6 us -> 1.5 us
    pallas_call x3 -> x2, Pallas kernels: 17.2 us -> 78.4 us  [the longest x1 61.2 us: mid(): pl.pallas_call(mid_kernel, out_shape=(shard, shard, shard, jax.ShapeDtype...]
    concatenate x3 -> x0, local copies, waits for them, and re-layouts: 28.5 us -> none  [the longest x1 25.3 us: local_step(): jnp.concatenate([w_new, w_edge, jnp.zeros(((OWN + 512) * LANES - SLICE -...]
    sub x2 -> x0, other arithmetic: 13.6 us -> none  [adam_update(): w_new = w_old - LEARN_RATE * m_hat / (jnp.sqrt(v_hat) + ADAM_EPS)]
    squeeze x7 -> x0, local copies, waits for them, and re-layouts: 12.9 us -> none  [local_step(): pieces.append(full[d, low - OWN_STARTS[d]:high - OWN_STARTS[d]])]
    slice x1 -> x0, local copies, waits for them, and re-layouts: 8.57 us -> none  [local_step(): w_chip = chip.reshape(1, -1)[:, :13824 * LANES + block].astype(jnp.bfloat16)]
where the time goes in v2:
time: 395 us
  Pallas kernels  391 us (99%)
    pallas_call x1, Pallas kernels, scatter(): pl.pallas_call(scatter_kernel, out_shape=(jax.ShapeDtypeStruct((WINDOW, L...  207 us
    pallas_call x1, Pallas kernels, gather(): pl.pallas_call(gather_kernel, out_shape=jax.ShapeDtypeStruct((2, 2, 2, 2,...  106 us
    pallas_call x1, Pallas kernels, mid(): pl.pallas_call(mid_kernel, out_shape=(shard, shard, shard, jax.ShapeDtype...  61.2 us
    pallas_call x1, Pallas kernels, finish(): pl.pallas_call(final_kernel, out_shape=tuple((shape(end - base) for base,...  17.2 us

profile of v2, /device:TPU:0, one launch (start us, length us, event | category | flops | bytes accessed | tf_op | source)
XLA Modules:
  0.0 394.7 jit_solution(9192927573134954400)
XLA Ops:
  0.6 0.9 reduce
  1.6 0.6 pad_bitcast_fusion.b_ref
  2.2 206.8 %shard_map.151 = (f32[7296,128]{1,0:T(8,128)}, f32[98304]{0:T(1024)}) custom-call(f32[32768,128]{1,0:T(8,128)} %bitcast.44, f32[32768,128]{1,0:T(8,128)} %bitcast.45, f32[22528,128]{1,0:T(8,128)} %bitcast.46, f32[22528,128]{1,0:T(8,128)} %bitcast.47, f32[128,128]{1,0:T(8,128)} %pad_bitcast_fusion.b_ref, f32[885488]{0:T(1024)} %m_ref.3, f32[885488]{0:T(1024)} %v_ref.3, ...), custom_call_target="tpu_custom_call" | custom-call | tf_op jit(solution)/shard_map/pallas_call | solution.py:267
  209.0 61.2 %shard_map.152 = (f32[885488]{0:T(1024)}, f32[885488]{0:T(1024)}, f32[885488]{0:T(1024)}, bf16[7200,128]{1,0:T(8,128)(2,1)}) custom-call(f32[7296,128]{1,0:T(8,128)} %get-tuple-element.21.tile_ref, f32[885488]{0:T(1024)} %m_ref.3, f32[885488]{0:T(1024)} %v_ref.3, f32[885488]{0:T(1024)} %w_ref.3, f32[98304]{0:T(1024)} %get-tuple-element.22.edge_ref), custom_call_target="tpu_custom_call" | custom-call | tf_op jit(solution)/shard_map/pallas_call | solution.py:484
  270.2 0.0 copy-start
  270.2 1.5 copy-done
  271.8 105.8 %shard_map.153 = bf16[2,2,2,2,7200,128]{5,4,3,2,1,0:T(8,128)(2,1)S(1)} custom-call(bf16[7200,128]{1,0:T(8,128)(2,1)S(1)} %copy-done), custom_call_target="tpu_custom_call" | custom-call | tf_op jit(solution)/shard_map/pallas_call | solution.py:358
  377.5 17.2 %shard_map.154 = (bf16[32768,128]{1,0:T(8,128)(2,1)}, bf16[32768,128]{1,0:T(8,128)(2,1)}, bf16[22528,128]{1,0:T(8,128)(2,1)}, bf16[22528,128]{1,0:T(8,128)(2,1)}...) custom-call(bf16[16,7200,128]{2,1,0:T(8,128)(2,1)S(1)} %bitcast.43), custom_call_target="tpu_custom_call" | custom-call | tf_op jit(solution)/shard_map/pallas_call | solution.py:590
Async XLA Ops:
  270.2 1.5 copy-start

commit v3 on v2

--- a/solution.py
+++ b/solution.py
@@ -30,7 +30,8 @@
 OWN_ITEMS = OWN_THIRD // OWN_CHUNK
 SIXTEEN = 16
 FINAL_LIMIT = 20000000
-GATHER_LIMIT = 6000000
+GATHER_LIMIT = 36000000
+MID_LIMIT = 64000000
 
 
 def floor_block(row):
@@ -69,9 +70,8 @@
 def adam_update(grad_mean, m_old, v_old, w_old):
     m_new = ADAM_BETA1 * m_old + (1.0 - ADAM_BETA1) * grad_mean
     v_new = ADAM_BETA2 * v_old + (1.0 - ADAM_BETA2) * (grad_mean * grad_mean)
-    m_hat = m_new / (1.0 - ADAM_BETA1 ** ADAM_STEP)
-    v_hat = v_new / (1.0 - ADAM_BETA2 ** ADAM_STEP)
-    w_new = w_old - LEARN_RATE * m_hat / (jnp.sqrt(v_hat) + ADAM_EPS)
+    scale = LEARN_RATE / (1.0 - ADAM_BETA1 ** ADAM_STEP)
+    w_new = w_old - scale * m_new / (jnp.sqrt(v_new * (1.0 / (1.0 - ADAM_BETA2 ** ADAM_STEP))) + ADAM_EPS)
     return m_new, v_new, w_new
 
 
@@ -358,7 +358,7 @@
     return pl.pallas_call(
         gather_kernel,
         out_shape=jax.ShapeDtypeStruct((2, 2, 2, 2, OWN, LANES), jnp.bfloat16),
-        in_specs=[pl.BlockSpec(memory_space=pltpu.VMEM)],
+        in_specs=[pl.BlockSpec(memory_space=pl.ANY)],
         out_specs=pl.BlockSpec(memory_space=pltpu.VMEM),
         scratch_shapes=[
             dma((3, OWN_ITEMS)), dma((3, OWN_ITEMS)), dma((3, OWN_ITEMS, 3)), dma((3, OWN_ITEMS, 3)), dma(()),
@@ -372,8 +372,8 @@
     return (outer * 2 + middle) * 4 + inner
 
 
-def for_blocks(start, length, action):
-    for base, end, tiles in TENSORS:
+def for_blocks(start, length, action, tensors=TENSORS):
+    for base, end, tiles in tensors:
         block = 8 * tiles
         low = (jnp.maximum(start, base) - base + block - 1) // block
         high = jnp.maximum(jnp.minimum(start + length, end) - base, 0) // block
@@ -392,13 +392,37 @@
 OWN_FLAT_ROWS = OWN + 512
 
 
-def lane_index():
-    return lax.broadcasted_iota(jnp.int32, (8, LANES), 1)
-
-
-def mid_kernel(tile_ref, m_ref, v_ref, w_ref, edge_ref, m_out, v_out, w_out, own_ref, flat, shifted, edged, aligned, tiled):
+def lane_index(rows=8):
+    return lax.broadcasted_iota(jnp.int32, (rows, LANES), 1)
+
+
+BATCH = 128
+BATCHES = SHARD_VREGS * 8 // BATCH
+CHUNK_BATCHES = 6
+CHUNKS = BATCHES // CHUNK_BATCHES
+CHUNK = CHUNK_BATCHES * BATCH * LANES
+
+
+def mid_kernel(tile_ref, m_ref, v_ref, w_ref, edge_ref, m_out, v_out, w_out, own_ref,
+               m_buf, v_buf, w_buf, flat, shifted, edged, aligned, in_sem, out_sem):
     device = device_index()
     start = window_start(device)
+    arrays = ((m_ref, m_buf, m_out), (v_ref, v_buf, v_out), (w_ref, w_buf, w_out))
+
+    def span(chunk):
+        return pl.ds(chunk * CHUNK, CHUNK if chunk < CHUNKS - 1 else SLICE - chunk * CHUNK)
+
+    def loads(chunk):
+        return [pltpu.make_async_copy(ref.at[span(chunk)], buf.at[span(chunk)], in_sem.at[n, chunk])
+                for n, (ref, buf, _) in enumerate(arrays)]
+
+    def stores(chunk):
+        return [pltpu.make_async_copy(buf.at[span(chunk)], out.at[span(chunk)], out_sem.at[n, chunk])
+                for n, (_, buf, out) in enumerate(arrays)]
+
+    for chunk in range(CHUNKS):
+        for copy in loads(chunk):
+            copy.start()
 
     def to_flat(row, tiles):
         for t in range(tiles):
@@ -409,90 +433,97 @@
     next_row = (device + 1) * (SLICE // 16) // 8
     shift = device * SLICE - first_row * LANES
     next_shift = (device + 1) * SLICE - next_row * LANES
-    lane = lane_index()
-
-    def mean_rows(row, amount):
-        here = flat[pl.ds(row, 8), :]
-        below = flat[pl.ds(row + 1, 8), :]
+
+    def mean_rows(row, amount, rows):
+        here = flat[pl.ds(row, rows), :]
+        below = flat[pl.ds(row + 1, rows), :]
         back = (LANES - amount) % LANES
-        return jnp.where(lane < LANES - amount, pltpu.roll(here, back, 1), pltpu.roll(below, back, 1))
-
-    def shard_step(n):
-        at = pl.ds(pl.multiple_of(n * 1024, 1024), 1024)
-        mean = mean_rows(first_row - start + n * 8, shift)
-        m_new, v_new, w_new = adam_update(mean, *(ref[at].reshape(8, LANES) for ref in (m_ref, v_ref, w_ref)))
-        m_out[at] = m_new.reshape(1024)
-        v_out[at] = v_new.reshape(1024)
-        w_out[at] = w_new.reshape(1024)
-        shifted[pl.ds(pl.multiple_of(PAD + n * 8, 8), 8), :] = pltpu.roll(w_new, shift, 1)
-
-    @pl.loop(0, SHARD_VREGS // 4)
-    def _(n):
-        for k in range(4):
-            shard_step(n * 4 + k)
-    for n in range(SHARD_VREGS // 4 * 4, SHARD_VREGS):
-        shard_step(n)
-
-    mean = mean_rows(first_row - start + SHARD_VREGS * 8, shift)
+        return jnp.where(lane_index(rows) < LANES - amount, pltpu.roll(here, back, 1), pltpu.roll(below, back, 1))
+
+    for chunk in range(CHUNKS):
+        for copy in loads(chunk):
+            copy.wait()
+
+        @pl.loop(chunk * CHUNK_BATCHES, (chunk + 1) * CHUNK_BATCHES)
+        def _(n):
+            at = pl.ds(pl.multiple_of(n * BATCH * LANES, BATCH * LANES), BATCH * LANES)
+            mean = mean_rows(first_row - start + n * BATCH, shift, BATCH)
+            new = adam_update(mean, *(buf[at].reshape(BATCH, LANES) for _, buf, _ in arrays))
+            for (_, buf, _), value in zip(arrays, new):
+                buf[at] = value.reshape(BATCH * LANES)
+            shifted[pl.ds(pl.multiple_of(PAD + n * BATCH, 8), BATCH), :] = pltpu.roll(new[2], shift, 1)
+
+        if chunk > 0:
+            for copy in stores(chunk - 1):
+                copy.start()
+
+    mean = mean_rows(first_row - start + SHARD_VREGS * 8, shift, 8)
     for r in range(TAIL_ROWS + 1):
         size = LANES if r < TAIL_ROWS else TAIL_LANES
         at = pl.ds(SHARD_VREGS * 1024 + r * LANES, size)
-        m_new, v_new, w_new = adam_update(
-            mean[r:r + 1, :size], *(ref[at].reshape(1, size) for ref in (m_ref, v_ref, w_ref)))
-        m_out[at] = m_new.reshape(size)
-        v_out[at] = v_new.reshape(size)
-        w_out[at] = w_new.reshape(size)
-        flat[pl.ds(FLAT_ROWS - 8 + r, 1), pl.ds(0, size)] = w_new
+        new = adam_update(mean[r:r + 1, :size], *(buf[at].reshape(1, size) for _, buf, _ in arrays))
+        for (_, buf, _), value in zip(arrays, new):
+            buf[at] = value.reshape(size)
+        flat[pl.ds(FLAT_ROWS - 8 + r, 1), pl.ds(0, size)] = new[2]
     shifted[pl.ds(PAD + SHARD_VREGS * 8, 8), :] = pltpu.roll(flat[pl.ds(FLAT_ROWS - 8, 8), :], shift, 1)
 
-    @pl.loop(0, EDGE_ROWS // 8)
+    @pl.loop(0, EDGE_ROWS // 64)
     def _(n):
-        mean = mean_rows(next_row - start + n * 8, next_shift)
-        old = (edge_ref[pl.ds(pl.multiple_of(k * EDGE + n * 1024, 1024), 1024)].reshape(8, LANES) for k in range(3))
-        edged[pl.ds(pl.multiple_of(PAD + n * 8, 8), 8), :] = pltpu.roll(adam_update(mean, *old)[2], next_shift, 1)
+        mean = mean_rows(next_row - start + n * 64, next_shift, 64)
+        old = (edge_ref[pl.ds(pl.multiple_of(k * EDGE + n * 8192, 1024), 8192)].reshape(64, LANES) for k in range(3))
+        edged[pl.ds(pl.multiple_of(PAD + n * 64, 8), 64), :] = pltpu.roll(adam_update(mean, *old)[2], next_shift, 1)
+
+    for copy in stores(CHUNKS - 1):
+        copy.start()
 
     own = own_start(device)
     skip = own - first_row
 
-    @pl.loop(0, SHARD_VREGS + 1)
+    @pl.loop(0, BATCHES + 1)
     def _(n):
-        row = PAD + skip + n * 8
-        aligned[pl.ds(pl.multiple_of(n * 8, 8), 8), :] = jnp.where(
-            lane >= shift, shifted[pl.ds(row, 8), :], shifted[pl.ds(row - 1, 8), :])
+        row = PAD + skip + n * BATCH
+        aligned[pl.ds(pl.multiple_of(n * BATCH, 8), BATCH), :] = jnp.where(
+            lane_index(BATCH) >= shift, shifted[pl.ds(row, BATCH), :], shifted[pl.ds(row - 1, BATCH), :])
     edged[pl.ds(PAD - 1, 1), :] = aligned[pl.ds(next_row - own, 1), :]
 
-    @pl.loop(0, EDGE_ROWS // 8)
+    @pl.loop(0, EDGE_ROWS // 64)
     def _(n):
-        row = PAD + n * 8
-        aligned[pl.ds(next_row - own + n * 8, 8), :] = jnp.where(
-            lane >= next_shift, edged[pl.ds(row, 8), :], edged[pl.ds(row - 1, 8), :])
+        row = PAD + n * 64
+        aligned[pl.ds(next_row - own + n * 64, 64), :] = jnp.where(
+            lane_index(64) >= next_shift, edged[pl.ds(row, 64), :], edged[pl.ds(row - 1, 64), :])
 
     def to_tile(row, tiles):
-        for t in range(tiles):
-            tiled[pl.ds(row + 8 * t, 8), :] = aligned[pl.ds(row + t, 8, stride=tiles), :]
-    for_blocks(own, OWN, to_tile)
-
-    @pl.loop(0, OWN // 32)
-    def _(n):
-        rows = pl.ds(pl.multiple_of(n * 32, 32), 32)
-        own_ref[rows, :] = tiled[rows, :].astype(jnp.bfloat16)
+        for t in range(0, tiles, 2):
+            both = [aligned[pl.ds(row + t + k, 8, stride=tiles), :] for k in range(2)]
+            own_ref[pl.ds(pl.multiple_of(row + 8 * t, 16), 16), :] = jnp.concatenate(both, axis=0).astype(jnp.bfloat16)
+
+    def plain(row, _):
+        own_ref[pl.ds(pl.multiple_of(row, 16), 16), :] = aligned[pl.ds(row, 16), :].astype(jnp.bfloat16)
+    for_blocks(own, OWN, to_tile, TENSORS[:4])
+    for_blocks(own, OWN, plain, ((*TENSORS[4][:2], 2),))
+
+    for chunk in range(CHUNKS):
+        for copy in stores(chunk):
+            copy.wait()
 
 
 def mid(mean_tiles, m, v, w, edges):
     vmem = pl.BlockSpec(memory_space=pltpu.VMEM)
+    any_spec = pl.BlockSpec(memory_space=pl.ANY)
     shard = jax.ShapeDtypeStruct((SLICE,), jnp.float32)
     return pl.pallas_call(
         mid_kernel,
         out_shape=(shard, shard, shard, jax.ShapeDtypeStruct((OWN, LANES), jnp.bfloat16)),
-        in_specs=[vmem] * 5, out_specs=(vmem,) * 4,
+        in_specs=[vmem, any_spec, any_spec, any_spec, vmem], out_specs=(any_spec, any_spec, any_spec, vmem),
         scratch_shapes=[
+            pltpu.VMEM((SLICE,), jnp.float32), pltpu.VMEM((SLICE,), jnp.float32), pltpu.VMEM((SLICE,), jnp.float32),
             pltpu.VMEM((FLAT_ROWS, LANES), jnp.float32),
             pltpu.VMEM((PAD + SHARD_VREGS * 8 + 8 + 512, LANES), jnp.float32),
             pltpu.VMEM((PAD + EDGE_ROWS, LANES), jnp.float32),
             pltpu.VMEM((OWN_FLAT_ROWS, LANES), jnp.float32),
-            pltpu.VMEM((OWN, LANES), jnp.float32),
+            pltpu.SemaphoreType.DMA((3, CHUNKS)), pltpu.SemaphoreType.DMA((3, CHUNKS)),
         ],
-        compiler_params=pltpu.CompilerParams(vmem_limit_bytes=60000000),
+        compiler_params=pltpu.CompilerParams(vmem_limit_bytes=MID_LIMIT),
     )(mean_tiles, m, v, w, edges)
 
 

time: 395 us -> 372 us (0.942)
  Pallas kernels: 391 us -> 359 us
  local copies, waits for them, and re-layouts: 2.14 us -> 11.5 us
    pallas_call x1, Pallas kernels: 61.2 us -> 19.2 us  [mid(): pl.pallas_call(mid_kernel, out_shape=(shard, shard, shard, jax.ShapeDtype...]
    pallas_call x1, Pallas kernels: 106 us -> 115 us  [gather(): pl.pallas_call(gather_kernel, out_shape=jax.ShapeDtypeStruct((2, 2, 2, 2,...]
    unnamed x2 -> x4, local copies, waits for them, and re-layouts: 1.5 us -> 10.9 us
where the time goes in v3:
time: 372 us
  Pallas kernels  359 us (97%)
  local copies, waits for them, and re-layouts  11.5 us (3%)
    pallas_call x1, Pallas kernels, scatter(): pl.pallas_call(scatter_kernel, out_shape=(jax.ShapeDtypeStruct((WINDOW, L...  207 us
    pallas_call x1, Pallas kernels, gather(): pl.pallas_call(gather_kernel, out_shape=jax.ShapeDtypeStruct((2, 2, 2, 2,...  115 us
    pallas_call x1, Pallas kernels, mid(): pl.pallas_call(mid_kernel, out_shape=(shard, shard, shard, jax.ShapeDtype...  19.2 us
    pallas_call x1, Pallas kernels, finish(): pl.pallas_call(final_kernel, out_shape=tuple((shape(end - base) for base,...  17.2 us
    unnamed x4, local copies, waits for them, and re-layouts  10.9 us

profile of v3, /device:TPU:0, one launch (start us, length us, event | category | flops | bytes accessed | tf_op | source)
XLA Modules:
  0.0 371.7 jit_solution(13142125587565818437)
XLA Ops:
  0.6 0.9 reduce
  1.6 0.6 pad_bitcast_fusion.b_ref
  2.2 206.8 %shard_map.151 = (f32[7296,128]{1,0:T(8,128)}, f32[98304]{0:T(1024)}) custom-call(f32[32768,128]{1,0:T(8,128)} %bitcast.44, f32[32768,128]{1,0:T(8,128)} %bitcast.45, f32[22528,128]{1,0:T(8,128)} %bitcast.46, f32[22528,128]{1,0:T(8,128)} %bitcast.47, f32[128,128]{1,0:T(8,128)} %pad_bitcast_fusion.b_ref, f32[885488]{0:T(1024)} %m_ref.3, f32[885488]{0:T(1024)} %v_ref.3, ...), custom_call_target="tpu_custom_call" | custom-call | tf_op jit(solution)/shard_map/pallas_call | solution.py:267
  209.0 19.2 %shard_map.152 = (f32[885488]{0:T(1024)}, f32[885488]{0:T(1024)}, f32[885488]{0:T(1024)}, bf16[7200,128]{1,0:T(8,128)(2,1)}) custom-call(f32[7296,128]{1,0:T(8,128)} %get-tuple-element.21.tile_ref, f32[885488]{0:T(1024)} %m_ref.3, f32[885488]{0:T(1024)} %v_ref.3, f32[885488]{0:T(1024)} %w_ref.3, f32[98304]{0:T(1024)} %get-tuple-element.22.edge_ref), custom_call_target="tpu_custom_call" | custom-call | tf_op jit(solution)/shard_map/pallas_call | solution.py:514
  228.3 0.0 copy-start.1
  228.3 1.5 copy-done.1
  229.8 115.3 %shard_map.153 = bf16[2,2,2,2,7200,128]{5,4,3,2,1,0:T(8,128)(2,1)} custom-call(bf16[7200,128]{1,0:T(8,128)(2,1)S(1)} %copy-done.1), custom_call_target="tpu_custom_call" | custom-call | tf_op jit(solution)/shard_map/pallas_call | solution.py:358
  345.1 0.0 copy-start
  345.1 9.4 %copy-done = bf16[2,2,2,2,7200,128]{5,4,3,2,1,0:T(8,128)(2,1)S(1)} copy-done((bf16[2,2,2,2,7200,128]{5,4,3,2,1,0:T(8,128)(2,1)S(1)}, bf16[2,2,2,2,7200,128]{5,4,3,2,1,0:T(8,128)(2,1)}, u32[]{:S(2)}) %copy-start) | copy-done | bytes 29491224
  354.5 17.2 %shard_map.154 = (bf16[32768,128]{1,0:T(8,128)(2,1)}, bf16[32768,128]{1,0:T(8,128)(2,1)}, bf16[22528,128]{1,0:T(8,128)(2,1)}, bf16[22528,128]{1,0:T(8,128)(2,1)}...) custom-call(bf16[16,7200,128]{2,1,0:T(8,128)(2,1)S(1)} %bitcast.43), custom_call_target="tpu_custom_call" | custom-call | tf_op jit(solution)/shard_map/pallas_call | solution.py:621
Async XLA Ops:
  228.3 1.5 copy-start.1
  345.1 9.4 %copy-start = (bf16[2,2,2,2,7200,128]{5,4,3,2,1,0:T(8,128)(2,1)S(1)}, bf16[2,2,2,2,7200,128]{5,4,3,2,1,0:T(8,128)(2,1)}, u32[]{:S(2)}) copy-start(bf16[2,2,2,2,7200,128]{5,4,3,2,1,0:T(8,128)(2,1)} %shard_map.153) | copy-start | bytes 88473600

commit v4 on v3

--- a/solution.py
+++ b/solution.py
@@ -19,25 +19,29 @@
 SLICE = 885488
 TENSORS = ((0, 32768, 8), (32768, 65536, 32), (65536, 88064, 22), (88064, 110592, 8), (110592, 110720, 1))
 ROWS = 110720
-UNIT = 128
-WINDOW = 7296
-THIRD = WINDOW // 3
-ITEMS = THIRD // UNIT
+VEC_BLOCK_ROWS = 128
+UNIT = 64
+WINDOW = 7232
+COUNTS = (38, 38, 37)
+FIRSTS = (0, 38, 76)
+ITEMS = max(COUNTS)
+LAG = 2
 EDGE = 32768
-OWN = 7200
+OWN = 7104
 OWN_THIRD = OWN // 3
-OWN_CHUNK = 160
+OWN_CHUNK = 64
 OWN_ITEMS = OWN_THIRD // OWN_CHUNK
+OWN_LAG = 2
 SIXTEEN = 16
 FINAL_LIMIT = 20000000
-GATHER_LIMIT = 36000000
+GATHER_LIMIT = 6000000
 MID_LIMIT = 64000000
 
 
 def floor_block(row):
     result = row
     for base, end, tiles in TENSORS:
-        block = 8 * tiles if tiles > 1 else UNIT
+        block = 8 * tiles if tiles > 1 else VEC_BLOCK_ROWS
         floored = base + (row - base) // block * block
         result = jnp.where((row >= base) & (row < end), floored, result)
     return result
@@ -52,7 +56,7 @@
     row = -(-index * SLICE // LANES)
     for base, end, tiles in TENSORS:
         if base <= row < end:
-            block = 8 * tiles if tiles > 1 else UNIT
+            block = 8 * tiles if tiles > 1 else VEC_BLOCK_ROWS
             return base + -(-(row - base) // block) * block
     return ROWS
 
@@ -108,7 +112,7 @@
 
 def scatter_kernel(e_ref, a_ref, f_ref, h_ref, b_ref, m_ref, v_ref, w_ref, out_ref, edge_ref,
                    part, recv0, recv1, recv2, mine, pair_send, pair_recv, mine_sem,
-                   send0, send1, send2, arrive0, arrive1, arrive2, out_sem, edge_send, edge_recv):
+                   send, arrive, out_sem, edge_send, edge_recv):
     z, y, x, core = position()
     chip = (z * 2 + y) * 2 + x
     device = chip * 2 + core
@@ -128,7 +132,16 @@
                 action(source.at[pl.ds(pl.multiple_of(row - base, UNIT), UNIT), :])
 
     def item_row(third, item):
-        return pl.multiple_of(third * THIRD + item * UNIT, UNIT)
+        return pl.multiple_of((FIRSTS[third] + item) * UNIT, UNIT)
+
+    def each_third(item, action):
+        for third in range(3):
+            if COUNTS[third] == ITEMS:
+                action(third)
+            else:
+                @pl.when(item < COUNTS[third])
+                def _():
+                    action(third)
 
     def start_pair(item):
         @pl.loop(0, 8)
@@ -136,12 +149,14 @@
             jz, jy, jx = j // 4, j // 2 % 2, j % 2
             other = ((z + jz) % 2 * 2 + (y + jy) % 2) * 2 + (x + jx) % 2
             start = window_start(other * 2 + 1 - core)
-            for third in range(3):
+
+            def action(third):
                 row = item_row(third, item)
                 from_source(start + row, lambda src: pltpu.make_async_remote_copy(
                     src_ref=src, dst_ref=part.at[jz, jy, jx, pl.ds(row, UNIT), :],
-                    send_sem=pair_send.at[third, item], recv_sem=pair_recv.at[third, item],
+                    send_sem=pair_send.at[third], recv_sem=pair_recv.at[third, item],
                     device_id=neighbour(3), device_id_type=MESH).start())
+            each_third(item, action)
 
     def start_mine(item, slot):
         @pl.loop(0, 8)
@@ -149,13 +164,14 @@
             jz, jy, jx = j // 4, j // 2 % 2, j % 2
             other = ((z + jz) % 2 * 2 + (y + jy) % 2) * 2 + (x + jx) % 2
             start = window_start(other * 2 + core)
-            for third in range(3):
-                row = item_row(third, item)
-                from_source(start + row, lambda src: pltpu.make_async_copy(
-                    src, mine.at[slot, third, jz, jy, jx], mine_sem.at[slot]).start())
-
-    def hop_copy(third, item, hop):
-        rows = pl.ds(item_row(third, item), UNIT)
+
+            def action(third):
+                from_source(start + item_row(third, item), lambda src: pltpu.make_async_copy(
+                    src, mine.at[slot, third, jz, jy, jx], mine_sem.at[slot, third]).start())
+            each_third(item, action)
+
+    def hop_copy(third, item, hop, whole=False):
+        rows = pl.ds(item_row(third, 0), COUNTS[third] * UNIT) if whole else pl.ds(item_row(third, item), UNIT)
         first, second, last = ORDERS[third]
         if hop == 0:
             index = tuple(1 if n == first else slice(None) for n in range(3))
@@ -168,91 +184,81 @@
             target = recv2.at[rows, :]
         return pltpu.make_async_remote_copy(
             src_ref=part.at[index + (rows, slice(None))], dst_ref=target,
-            send_sem=(send0, send1, send2)[hop].at[third, item], recv_sem=(arrive0, arrive1, arrive2)[hop].at[third, item],
+            send_sem=send.at[third, hop], recv_sem=arrive.at[third, hop, item],
             device_id=neighbour(ORDERS[third][hop]), device_id_type=MESH)
 
-    def pair_all(third, item):
-        block = part.at[:, :, :, pl.ds(item_row(third, item), UNIT), :]
+    def pair_all(third, item, whole=False):
+        rows = pl.ds(item_row(third, 0), COUNTS[third] * UNIT) if whole else pl.ds(item_row(third, item), UNIT)
+        block = part.at[:, :, :, rows, :]
         return pltpu.make_async_remote_copy(
-            src_ref=block, dst_ref=block, send_sem=pair_send.at[third, item], recv_sem=pair_recv.at[third, item],
+            src_ref=block, dst_ref=block, send_sem=pair_send.at[third], recv_sem=pair_recv.at[third, item],
             device_id=neighbour(3), device_id_type=MESH)
 
-    def out_copy(third, item):
+    def out_copy(third, item, whole=False):
+        rows = pl.ds(item_row(third, 0), COUNTS[third] * UNIT) if whole else pl.ds(item_row(third, item), UNIT)
+        return pltpu.make_async_copy(part.at[0, 0, 0, rows, :], out_ref.at[rows, :], out_sem.at[third])
+
+    start_pair(0)
+    start_mine(0, 0)
+
+    def stage0(item, third):
         rows = pl.ds(item_row(third, item), UNIT)
-        return pltpu.make_async_copy(part.at[0, 0, 0, rows, :], out_ref.at[rows, :], out_sem.at[third, item])
-
-    start_mine(0, 0)
-    start_pair(0)
-    start_pair(1)
-
-    @pl.loop(0, ITEMS + 4)
+        slot = item % 2
+        pltpu.make_async_copy(mine.at[slot, third], mine.at[slot, third], mine_sem.at[slot, third]).wait()
+        pair_all(third, item).wait_recv()
+        for j in range(8):
+            index = (j // 4, j // 2 % 2, j % 2)
+            part[index + (rows, slice(None))] += mine[(slot, third) + index]
+        hop_copy(third, item, 0).start()
+
+    def stage1(item, third):
+        rows = pl.ds(item_row(third, item), UNIT)
+        hop_copy(third, item, 0).wait_recv()
+        first = ORDERS[third][0]
+        for j in range(4):
+            pair = [j // 2, j % 2]
+            index = tuple(pair[:first] + [0] + pair[first:])
+            part[index + (rows, slice(None))] += recv0[j // 2, j % 2, rows, :]
+        hop_copy(third, item, 1).start()
+
+    def stage2(item, third):
+        rows = pl.ds(item_row(third, item), UNIT)
+        hop_copy(third, item, 1).wait_recv()
+        last = ORDERS[third][2]
+        for j in range(2):
+            index = tuple(j if n == last else 0 for n in range(3))
+            part[index + (rows, slice(None))] += recv1[j, rows, :]
+        hop_copy(third, item, 2).start()
+
+    def stage3(item, third):
+        rows = pl.ds(item_row(third, item), UNIT)
+        hop_copy(third, item, 2).wait_recv()
+        part[0, 0, 0, rows, :] = (part[0, 0, 0, rows, :] + recv2[rows, :]) / SIXTEEN
+
+    stages = ((0, stage0), (LAG, stage1), (2 * LAG, stage2), (3 * LAG, stage3),
+              (3 * LAG + 1, lambda item, third: out_copy(third, item).start()))
+
+    @pl.loop(0, ITEMS + stages[-1][0])
     def _(step):
-        @pl.when(step < ITEMS)
-        def _():
-            slot = step % 2
-
-            @pl.when(step + 1 < ITEMS)
+        for delay, stage in stages:
+            if delay == 0:
+                @pl.when(step + 1 < ITEMS)
+                def _():
+                    start_pair(step + 1)
+
+            @pl.when((step >= delay) & (step < ITEMS + delay))
             def _():
-                start_mine(step + 1, 1 - slot)
-
-            @pl.when(step + 2 < ITEMS)
-            def _():
-                start_pair(step + 2)
-
-            pltpu.make_async_copy(mine.at[slot], mine.at[slot], mine_sem.at[slot]).wait()
-            for third in range(3):
-                rows = pl.ds(item_row(third, step), UNIT)
-                pair_all(third, step).wait_recv()
-                for j in range(8):
-                    index = (j // 4, j // 2 % 2, j % 2)
-                    part[index + (rows, slice(None))] += mine[(slot, third) + index]
-                hop_copy(third, step, 0).start()
-
-        @pl.when((step >= 1) & (step < ITEMS + 1))
-        def _():
-            item = step - 1
-            for third in range(3):
-                rows = pl.ds(item_row(third, item), UNIT)
-                hop_copy(third, item, 0).wait_recv()
-                first = ORDERS[third][0]
-                for j in range(4):
-                    pair = [j // 2, j % 2]
-                    index = tuple(pair[:first] + [0] + pair[first:])
-                    part[index + (rows, slice(None))] += recv0[j // 2, j % 2, rows, :]
-                hop_copy(third, item, 1).start()
-
-        @pl.when((step >= 2) & (step < ITEMS + 2))
-        def _():
-            item = step - 2
-            for third in range(3):
-                rows = pl.ds(item_row(third, item), UNIT)
-                hop_copy(third, item, 1).wait_recv()
-                last = ORDERS[third][2]
-                for j in range(2):
-                    index = tuple(j if n == last else 0 for n in range(3))
-                    part[index + (rows, slice(None))] += recv1[j, rows, :]
-                hop_copy(third, item, 2).start()
-
-        @pl.when((step >= 3) & (step < ITEMS + 3))
-        def _():
-            item = step - 3
-            for third in range(3):
-                rows = pl.ds(item_row(third, item), UNIT)
-                hop_copy(third, item, 2).wait_recv()
-                part[0, 0, 0, rows, :] = (part[0, 0, 0, rows, :] + recv2[rows, :]) / SIXTEEN
-
-        @pl.when(step >= 4)
-        def _():
-            for third in range(3):
-                out_copy(third, step - 4).start()
-
-    @pl.loop(0, ITEMS)
-    def _(item):
-        for third in range(3):
-            pair_all(third, item).wait_send()
-            for hop in range(3):
-                hop_copy(third, item, hop).wait_send()
-            out_copy(third, item).wait()
+                each_third(step - delay, functools.partial(stage, step - delay))
+            if delay == 0:
+                @pl.when(step + 1 < ITEMS)
+                def _():
+                    start_mine(step + 1, (step + 1) % 2)
+
+    for third in range(3):
+        pair_all(third, 0, True).wait_send()
+        for hop in range(3):
+            hop_copy(third, 0, hop, True).wait_send()
+        out_copy(third, 0, True).wait()
 
     for n, ref in enumerate((m_ref, v_ref, w_ref)):
         pltpu.make_async_remote_copy(
@@ -275,27 +281,24 @@
             pltpu.VMEM((2, WINDOW, LANES), jnp.float32),
             pltpu.VMEM((WINDOW, LANES), jnp.float32),
             pltpu.VMEM((2, 3, 2, 2, 2, UNIT, LANES), jnp.float32),
-            dma((3, ITEMS)), dma((3, ITEMS)), dma((2,)),
-            dma((3, ITEMS)), dma((3, ITEMS)), dma((3, ITEMS)),
-            dma((3, ITEMS)), dma((3, ITEMS)), dma((3, ITEMS)),
-            dma((3, ITEMS)), dma((3,)), dma((3,)),
+            dma((3,)), dma((3, ITEMS)), dma((2, 3)),
+            dma((3, 3)), dma((3, 3, ITEMS)), dma((3,)), dma((3,)), dma((3,)),
         ],
         compiler_params=pltpu.CompilerParams(has_side_effects=True, vmem_limit_bytes=67043328),
     )(*grads, m, v, w)
 
 
-def gather_kernel(w_ref, full_ref, pair_send, pair_recv, send, arrive, own_sem):
+def gather_kernel(w_ref, full_ref, pair_send, pair_recv, send, arrive):
     z, y, x, core = position()
     here = (z, y, x)
 
-    def rows_of(third, item):
+    def rows_of(third, item, whole=False):
+        if whole:
+            return pl.ds(third * OWN_THIRD, OWN_THIRD)
         return pl.ds(pl.multiple_of(third * OWN_THIRD + item * OWN_CHUNK, OWN_CHUNK), OWN_CHUNK)
 
-    own = pltpu.make_async_copy(w_ref, full_ref.at[z, y, x, core], own_sem)
-    own.start()
-
-    def copy(third, item, hop):
-        rows = rows_of(third, item)
+    def copy(third, item, hop, whole=False):
+        rows = rows_of(third, item, whole)
         order = ORDERS[third]
         if hop == 0:
             source = w_ref.at[rows, :]
@@ -304,39 +307,45 @@
             index = tuple(slice(None) if n in order[:hop] else here[n] for n in range(3))
             source = target = full_ref.at[index + (core, rows, slice(None))]
         return pltpu.make_async_remote_copy(
-            src_ref=source, dst_ref=target, send_sem=send.at[third, item, hop], recv_sem=arrive.at[third, item, hop],
+            src_ref=source, dst_ref=target, send_sem=send.at[third, hop], recv_sem=arrive.at[third, item, hop],
             device_id=neighbour(order[hop]), device_id_type=MESH)
 
     def arrival(third, item, hop):
-        rows = rows_of(third, item)
         order = ORDERS[third]
         index = tuple(slice(None) if n in order[:hop] else (1 - here[n] if n == order[hop] else here[n]) for n in range(3))
-        block = full_ref.at[index + (core, rows, slice(None))]
+        block = full_ref.at[index + (core, rows_of(third, item), slice(None))]
         return pltpu.make_async_remote_copy(
-            src_ref=block, dst_ref=block, send_sem=send.at[third, item, hop], recv_sem=arrive.at[third, item, hop],
+            src_ref=block, dst_ref=block, send_sem=send.at[third, hop], recv_sem=arrive.at[third, item, hop],
             device_id=neighbour(order[hop]), device_id_type=MESH)
 
-    def pair(third, item, side):
-        block = full_ref.at[:, :, :, side, rows_of(third, item), :]
+    def pair(third, item, side, whole=False):
+        block = full_ref.at[:, :, :, side, rows_of(third, item, whole), :]
         return pltpu.make_async_remote_copy(
-            src_ref=block, dst_ref=block, send_sem=pair_send.at[third, item], recv_sem=pair_recv.at[third, item],
+            src_ref=block, dst_ref=block, send_sem=pair_send.at[third], recv_sem=pair_recv.at[third, item],
             device_id=neighbour(3), device_id_type=MESH)
 
-    for third in range(3):
-        copy(third, 0, 0).start()
-    own.wait()
-
-    @pl.loop(0, OWN_ITEMS + 3)
+    for item in range(OWN_LAG):
+        for third in range(3):
+            copy(third, item, 0).start()
+
+    @pl.loop(0, OWN // OWN_CHUNK)
+    def _(n):
+        rows = pl.ds(pl.multiple_of(n * OWN_CHUNK, OWN_CHUNK), OWN_CHUNK)
+        full_ref[z, y, x, core, rows, :] = w_ref[rows, :]
+
+    @pl.loop(0, OWN_ITEMS + 2 * OWN_LAG)
     def _(step):
-        @pl.when(step + 1 < OWN_ITEMS)
+        @pl.when(step + OWN_LAG < OWN_ITEMS)
         def _():
             for third in range(3):
-                copy(third, step + 1, 0).start()
+                copy(third, step + OWN_LAG, 0).start()
 
         for hop in range(1, 4):
-            @pl.when((step >= hop - 1) & (step < OWN_ITEMS + hop - 1))
+            delay = (hop - 1) * OWN_LAG
+
+            @pl.when((step >= delay) & (step < OWN_ITEMS + delay))
             def _():
-                item = step - (hop - 1)
+                item = step - delay
                 for third in range(3):
                     arrival(third, item, hop - 1).wait_recv()
                     if hop < 3:
@@ -348,9 +357,10 @@
     def _(item):
         for third in range(3):
             pair(third, item, 1 - core).wait_recv()
-            pair(third, item, core).wait_send()
-            for hop in range(3):
-                copy(third, item, hop).wait_send()
+    for third in range(3):
+        pair(third, 0, core, True).wait_send()
+        for hop in range(3):
+            copy(third, 0, hop, True).wait_send()
 
 
 def gather(w_own):
@@ -358,10 +368,10 @@
     return pl.pallas_call(
         gather_kernel,
         out_shape=jax.ShapeDtypeStruct((2, 2, 2, 2, OWN, LANES), jnp.bfloat16),
-        in_specs=[pl.BlockSpec(memory_space=pl.ANY)],
+        in_specs=[pl.BlockSpec(memory_space=pltpu.VMEM)],
         out_specs=pl.BlockSpec(memory_space=pltpu.VMEM),
         scratch_shapes=[
-            dma((3, OWN_ITEMS)), dma((3, OWN_ITEMS)), dma((3, OWN_ITEMS, 3)), dma((3, OWN_ITEMS, 3)), dma(()),
+            dma((3,)), dma((3, OWN_ITEMS)), dma((3, 3)), dma((3, OWN_ITEMS, 3)),
         ],
         compiler_params=pltpu.CompilerParams(has_side_effects=True, vmem_limit_bytes=GATHER_LIMIT),
     )(w_own)
@@ -542,9 +552,11 @@
 CHIP_COUNTS = tuple((end - base) // 8 for base, end, _ in TENSORS[:4])
 CHIP_ROWS = sum(CHIP_COUNTS)
 CHIP_SIZE = CHIP_ROWS * LANES + VEC_BLOCK
-
-
-def final_kernel(full_ref, e_out, a_out, f_out, h_out, vec_out, chip_out, block, flat, vec, out_sem, block_sem):
+CHIP_PARTS = 6
+CHIP_PART = CHIP_SIZE // 16384 // CHIP_PARTS * 16384
+
+
+def final_kernel(full_ref, e_out, a_out, f_out, h_out, vec_out, chip_ref, chip_out, flat, vec, out_sem, chip_sem):
     outs = (e_out, a_out, f_out, h_out)
     chip = device_index() // 2
     copies = []
@@ -565,21 +577,21 @@
         base, _, tiles = TENSORS[tensor]
         step = 16 * tiles
 
+        begin = base + chip * rows
+        slot, low, bound = jnp.int32(0), jnp.int32(0), jnp.int32(OWN_STARTS[1])
+        for d in range(1, SIXTEEN):
+            inside = begin >= OWN_STARTS[d]
+            slot = jnp.where(inside, d, slot)
+            low = jnp.where(inside, OWN_STARTS[d], low)
+            bound = jnp.where(inside, OWN_STARTS[d + 1], bound)
+
         @pl.loop(0, rows // step)
         def _(n):
-            row = base + chip * rows + n * step
-            slot = jnp.int32(0)
-            low = jnp.int32(0)
-            for d in range(1, SIXTEEN):
-                slot = jnp.where(row >= OWN_STARTS[d], d, slot)
-                low = jnp.where(row >= OWN_STARTS[d], OWN_STARTS[d], low)
-            second = row + 8 * tiles
-            slot2 = jnp.int32(0)
-            low2 = jnp.int32(0)
-            for d in range(1, SIXTEEN):
-                slot2 = jnp.where(second >= OWN_STARTS[d], d, slot2)
-                low2 = jnp.where(second >= OWN_STARTS[d], OWN_STARTS[d], low2)
-            for half, (at_slot, at_row) in enumerate(((slot, row - low), (slot2, second - low2))):
+            for half in range(2):
+                row = begin + n * step + half * 8 * tiles
+                following = row >= bound
+                at_slot = jnp.where(following, slot + 1, slot)
+                at_row = row - jnp.where(following, bound, low)
                 for t in range(0, tiles, 2):
                     value = full_ref[at_slot, pl.ds(pl.multiple_of(at_row + 8 * t, 16), 16), :].astype(jnp.float32)
                     for k in range(2):
@@ -596,20 +608,28 @@
         flat[pl.ds(CHIP_ROWS + n * 8, 8), :] = jnp.where(
             lane < LANES - amount, pltpu.roll(here, back, 1), pltpu.roll(below, back, 1))
 
-    @pl.loop(0, CHIP_SIZE // 4096)
-    def _(n):
-        for k in range(4):
-            chip_out[:, pl.ds(pl.multiple_of(n * 4096 + k * 1024, 1024), 1024)] = flat[
-                pl.ds(pl.multiple_of(n * 32 + k * 8, 8), 8), :].reshape(1, 1024).astype(jnp.bfloat16)
-    for n in range(CHIP_SIZE // 4096 * 4, CHIP_SIZE // 1024):
-        chip_out[:, n * 1024:(n + 1) * 1024] = flat[n * 8:n * 8 + 8, :].reshape(1, 1024).astype(jnp.bfloat16)
+    def part_copy(part):
+        span = pl.ds(part * CHIP_PART, CHIP_PART if part < CHIP_PARTS - 1 else CHIP_SIZE - part * CHIP_PART)
+        return pltpu.make_async_copy(chip_out.at[:, span], chip_ref.at[:, span], chip_sem.at[part])
+
+    for part in range(CHIP_PARTS):
+        @pl.loop(part * CHIP_PART // 16384, (part + 1) * CHIP_PART // 16384)
+        def _(n):
+            chip_out[:, pl.ds(pl.multiple_of(n * 16384, 16384), 16384)] = flat[
+                pl.ds(pl.multiple_of(n * 128, 128), 128), :].reshape(1, 16384).astype(jnp.bfloat16)
+        if part > 0:
+            part_copy(part - 1).start()
     done = CHIP_SIZE // 1024 * 1024
     rows = (CHIP_SIZE - done) // LANES
     last = CHIP_SIZE - done - rows * LANES
     first = done // LANES
+    chip_out[:, CHIP_PARTS * CHIP_PART:done] = flat[CHIP_PARTS * CHIP_PART // LANES:first, :].reshape(
+        1, done - CHIP_PARTS * CHIP_PART).astype(jnp.bfloat16)
     chip_out[:, done:done + rows * LANES] = flat[first:first + rows, :].reshape(1, rows * LANES).astype(jnp.bfloat16)
     chip_out[:, CHIP_SIZE - last:] = flat[first + rows:first + rows + 1, :last].astype(jnp.bfloat16)
-
+    part_copy(CHIP_PARTS - 1).start()
+    for part in range(CHIP_PARTS):
+        part_copy(part).wait()
     for copy in copies:
         copy.wait()
 
@@ -622,12 +642,12 @@
         final_kernel,
         out_shape=tuple(shape(end - base) for base, end, _ in TENSORS[:4]) + (
             jax.ShapeDtypeStruct((1, VEC_WIDTH), jnp.bfloat16), jax.ShapeDtypeStruct((1, CHIP_SIZE), jnp.bfloat16)),
-        in_specs=[vmem], out_specs=(any_spec,) * 4 + (vmem, vmem),
+        in_specs=[vmem], out_specs=(any_spec,) * 4 + (vmem, any_spec),
         scratch_shapes=[
-            pltpu.VMEM((16, LANES), jnp.bfloat16),
+            pltpu.VMEM((1, CHIP_SIZE), jnp.bfloat16),
             pltpu.VMEM((CHIP_ROWS + 16, LANES), jnp.float32),
             pltpu.VMEM((120, LANES), jnp.float32),
-            pltpu.SemaphoreType.DMA((len(PIECES),)), pltpu.SemaphoreType.DMA(()),
+            pltpu.SemaphoreType.DMA((len(PIECES),)), pltpu.SemaphoreType.DMA((CHIP_PARTS,)),
         ],
         compiler_params=pltpu.CompilerParams(vmem_limit_bytes=FINAL_LIMIT),
     )(full)
@@ -637,7 +657,7 @@
     def local_step(g_embed, g_attn, g_ffn_in, g_ffn_out, g_vec, m_shard, v_shard, w_shard):
         matrices = (g_embed, g_attn, g_ffn_in, g_ffn_out)
         grads = [to_tiles(g[0] if g.ndim == 3 else g[0, 0]) for g in matrices]
-        grads.append(jnp.pad(g_vec.reshape(-1), (0, UNIT * LANES - VEC_WIDTH)).reshape(UNIT, LANES))
+        grads.append(jnp.pad(g_vec.reshape(-1), (0, VEC_BLOCK_ROWS * LANES - VEC_WIDTH)).reshape(VEC_BLOCK_ROWS, LANES))
         mean_tiles, edges = scatter(grads, m_shard, v_shard, w_shard)
         m_new, v_new, w_new, w_own = mid(mean_tiles, m_shard, v_shard, w_shard, edges)
         full = gather(w_own).reshape(SIXTEEN, OWN, LANES)

time: 372 us -> 347 us (0.933)
  Pallas kernels: 359 us -> 343 us
  local copies, waits for them, and re-layouts: 11.5 us -> 2.12 us
    pallas_call x1, Pallas kernels: 115 us -> 105 us  [gather(): pl.pallas_call(gather_kernel, out_shape=jax.ShapeDtypeStruct((2, 2, 2, 2,...]
    unnamed x4 -> x2, local copies, waits for them, and re-layouts: 10.9 us -> 1.49 us
    pallas_call x1, Pallas kernels: 17.2 us -> 12.3 us  [finish(): pl.pallas_call(final_kernel, out_shape=tuple((shape(end - base) for base,...]
where the time goes in v4:
time: 347 us
  Pallas kernels  343 us (99%)
    pallas_call x1, Pallas kernels, scatter(): pl.pallas_call(scatter_kernel, out_shape=(jax.ShapeDtypeStruct((WINDOW, L...  206 us
    pallas_call x1, Pallas kernels, gather(): pl.pallas_call(gather_kernel, out_shape=jax.ShapeDtypeStruct((2, 2, 2, 2,...  105 us
    pallas_call x1, Pallas kernels, mid(): pl.pallas_call(mid_kernel, out_shape=(shard, shard, shard, jax.ShapeDtype...  19.2 us
    pallas_call x1, Pallas kernels, finish(): pl.pallas_call(final_kernel, out_shape=tuple((shape(end - base) for base,...  12.3 us

profile of v4, /device:TPU:0, one launch (start us, length us, event | category | flops | bytes accessed | tf_op | source)
XLA Modules:
  0.0 346.7 jit_solution(16442526332336964135)
XLA Ops:
  0.6 0.9 reduce
  1.6 0.6 pad_bitcast_fusion.b_ref
  2.2 206.4 %shard_map.151 = (f32[7232,128]{1,0:T(8,128)}, f32[98304]{0:T(1024)}) custom-call(f32[32768,128]{1,0:T(8,128)} %bitcast.44, f32[32768,128]{1,0:T(8,128)} %bitcast.45, f32[22528,128]{1,0:T(8,128)} %bitcast.46, f32[22528,128]{1,0:T(8,128)} %bitcast.47, f32[128,128]{1,0:T(8,128)} %pad_bitcast_fusion.b_ref, f32[885488]{0:T(1024)} %m_ref.3, f32[885488]{0:T(1024)} %v_ref.3, ...), custom_call_target="tpu_custom_call" | custom-call | tf_op jit(solution)/shard_map/pallas_call | solution.py:273
  208.6 19.2 %shard_map.152 = (f32[885488]{0:T(1024)}, f32[885488]{0:T(1024)}, f32[885488]{0:T(1024)}, bf16[7104,128]{1,0:T(8,128)(2,1)}) custom-call(f32[7232,128]{1,0:T(8,128)} %get-tuple-element.21.tile_ref, f32[885488]{0:T(1024)} %m_ref.3, f32[885488]{0:T(1024)} %v_ref.3, f32[885488]{0:T(1024)} %w_ref.3, f32[98304]{0:T(1024)} %get-tuple-element.22.edge_ref), custom_call_target="tpu_custom_call" | custom-call | tf_op jit(solution)/shard_map/pallas_call | solution.py:524
  227.9 0.0 copy-start
  227.9 1.5 copy-done
  229.4 105.0 %shard_map.153 = bf16[2,2,2,2,7104,128]{5,4,3,2,1,0:T(8,128)(2,1)S(1)} custom-call(bf16[7104,128]{1,0:T(8,128)(2,1)S(1)} %copy-done), custom_call_target="tpu_custom_call" | custom-call | tf_op jit(solution)/shard_map/pallas_call | solution.py:368
  334.4 12.3 %shard_map.154 = (bf16[32768,128]{1,0:T(8,128)(2,1)}, bf16[32768,128]{1,0:T(8,128)(2,1)}, bf16[22528,128]{1,0:T(8,128)(2,1)}, bf16[22528,128]{1,0:T(8,128)(2,1)}...) custom-call(bf16[16,7104,128]{2,1,0:T(8,128)(2,1)S(1)} %bitcast.43), custom_call_target="tpu_custom_call" | custom-call | tf_op jit(solution)/shard_map/pallas_call | solution.py:641
Async XLA Ops:
  227.9 1.5 copy-start

commit v5 on v4

--- a/solution.py
+++ b/solution.py
@@ -21,8 +21,9 @@
 ROWS = 110720
 VEC_BLOCK_ROWS = 128
 UNIT = 64
-WINDOW = 7232
-COUNTS = (38, 38, 37)
+GROUP = 128
+WINDOW = 7296
+COUNTS = (38, 38, 38)
 FIRSTS = (0, 38, 76)
 ITEMS = max(COUNTS)
 LAG = 2
@@ -49,7 +50,7 @@
 
 def window_start(index):
     row = floor_block(index * (SLICE // 16) // 8)
-    return jnp.minimum(row // UNIT * UNIT, ROWS - WINDOW)
+    return jnp.minimum(row // GROUP * GROUP, ROWS - WINDOW)
 
 
 def own_start_static(index):
@@ -126,49 +127,35 @@
             device_id=(before // 8, before // 4 % 2, before % 4), device_id_type=MESH).start()
 
     def from_source(row, action):
-        for source, (base, end, _) in zip(sources, TENSORS):
-            @pl.when((row >= base) & (row < end))
-            def _():
-                action(source.at[pl.ds(pl.multiple_of(row - base, UNIT), UNIT), :])
+        def choose(low, high):
+            if high - low == 1:
+                action(sources[low].at[pl.ds(pl.multiple_of(row - TENSORS[low][0], GROUP), GROUP), :])
+                return
+            middle = (low + high) // 2
+            lax.cond(row < TENSORS[middle][0], lambda: choose(low, middle), lambda: choose(middle, high))
+        choose(0, len(sources))
 
     def item_row(third, item):
         return pl.multiple_of((FIRSTS[third] + item) * UNIT, UNIT)
 
-    def each_third(item, action):
-        for third in range(3):
-            if COUNTS[third] == ITEMS:
-                action(third)
-            else:
-                @pl.when(item < COUNTS[third])
-                def _():
-                    action(third)
-
-    def start_pair(item):
+    def group_row(third, group):
+        return pl.multiple_of(FIRSTS[third] * UNIT + group * GROUP, GROUP)
+
+    def start_group(group, slot):
         @pl.loop(0, 8)
         def _(j):
             jz, jy, jx = j // 4, j // 2 % 2, j % 2
             other = ((z + jz) % 2 * 2 + (y + jy) % 2) * 2 + (x + jx) % 2
-            start = window_start(other * 2 + 1 - core)
-
-            def action(third):
-                row = item_row(third, item)
-                from_source(start + row, lambda src: pltpu.make_async_remote_copy(
-                    src_ref=src, dst_ref=part.at[jz, jy, jx, pl.ds(row, UNIT), :],
-                    send_sem=pair_send.at[third], recv_sem=pair_recv.at[third, item],
+            theirs = window_start(other * 2 + 1 - core)
+            ours = window_start(other * 2 + core)
+            for third in range(3):
+                row = group_row(third, group)
+                from_source(theirs + row, lambda src: pltpu.make_async_remote_copy(
+                    src_ref=src, dst_ref=part.at[jz, jy, jx, pl.ds(row, GROUP), :],
+                    send_sem=pair_send.at[third], recv_sem=pair_recv.at[third, group],
                     device_id=neighbour(3), device_id_type=MESH).start())
-            each_third(item, action)
-
-    def start_mine(item, slot):
-        @pl.loop(0, 8)
-        def _(j):
-            jz, jy, jx = j // 4, j // 2 % 2, j % 2
-            other = ((z + jz) % 2 * 2 + (y + jy) % 2) * 2 + (x + jx) % 2
-            start = window_start(other * 2 + core)
-
-            def action(third):
-                from_source(start + item_row(third, item), lambda src: pltpu.make_async_copy(
+                from_source(ours + row, lambda src: pltpu.make_async_copy(
                     src, mine.at[slot, third, jz, jy, jx], mine_sem.at[slot, third]).start())
-            each_third(item, action)
 
     def hop_copy(third, item, hop, whole=False):
         rows = pl.ds(item_row(third, 0), COUNTS[third] * UNIT) if whole else pl.ds(item_row(third, item), UNIT)
@@ -187,28 +174,32 @@
             send_sem=send.at[third, hop], recv_sem=arrive.at[third, hop, item],
             device_id=neighbour(ORDERS[third][hop]), device_id_type=MESH)
 
-    def pair_all(third, item, whole=False):
-        rows = pl.ds(item_row(third, 0), COUNTS[third] * UNIT) if whole else pl.ds(item_row(third, item), UNIT)
+    def pair_all(third, group, whole=False):
+        rows = pl.ds(FIRSTS[third] * UNIT, COUNTS[third] * UNIT) if whole else pl.ds(group_row(third, group), GROUP)
         block = part.at[:, :, :, rows, :]
         return pltpu.make_async_remote_copy(
-            src_ref=block, dst_ref=block, send_sem=pair_send.at[third], recv_sem=pair_recv.at[third, item],
+            src_ref=block, dst_ref=block, send_sem=pair_send.at[third], recv_sem=pair_recv.at[third, group],
             device_id=neighbour(3), device_id_type=MESH)
 
     def out_copy(third, item, whole=False):
         rows = pl.ds(item_row(third, 0), COUNTS[third] * UNIT) if whole else pl.ds(item_row(third, item), UNIT)
         return pltpu.make_async_copy(part.at[0, 0, 0, rows, :], out_ref.at[rows, :], out_sem.at[third])
 
-    start_pair(0)
-    start_mine(0, 0)
+    start_group(0, 0)
 
     def stage0(item, third):
         rows = pl.ds(item_row(third, item), UNIT)
-        slot = item % 2
-        pltpu.make_async_copy(mine.at[slot, third], mine.at[slot, third], mine_sem.at[slot, third]).wait()
-        pair_all(third, item).wait_recv()
+        group = item // 2
+        slot = group % 2
+
+        @pl.when(item % 2 == 0)
+        def _():
+            pltpu.make_async_copy(mine.at[slot, third], mine.at[slot, third], mine_sem.at[slot, third]).wait()
+            pair_all(third, group).wait_recv()
+        within = pl.ds(pl.multiple_of(item % 2 * UNIT, UNIT), UNIT)
         for j in range(8):
             index = (j // 4, j // 2 % 2, j % 2)
-            part[index + (rows, slice(None))] += mine[(slot, third) + index]
+            part[index + (rows, slice(None))] += mine[(slot, third) + index + (within, slice(None))]
         hop_copy(third, item, 0).start()
 
     def stage1(item, third):
@@ -241,18 +232,14 @@
     @pl.loop(0, ITEMS + stages[-1][0])
     def _(step):
         for delay, stage in stages:
-            if delay == 0:
-                @pl.when(step + 1 < ITEMS)
-                def _():
-                    start_pair(step + 1)
-
             @pl.when((step >= delay) & (step < ITEMS + delay))
             def _():
-                each_third(step - delay, functools.partial(stage, step - delay))
-            if delay == 0:
-                @pl.when(step + 1 < ITEMS)
-                def _():
-                    start_mine(step + 1, (step + 1) % 2)
+                for third in range(3):
+                    stage(step - delay, third)
+
+        @pl.when((step % 2 == 0) & (step + 2 < ITEMS))
+        def _():
+            start_group(step // 2 + 1, (step // 2 + 1) % 2)
 
     for third in range(3):
         pair_all(third, 0, True).wait_send()
@@ -280,8 +267,8 @@
             pltpu.VMEM((2, 2, WINDOW, LANES), jnp.float32),
             pltpu.VMEM((2, WINDOW, LANES), jnp.float32),
             pltpu.VMEM((WINDOW, LANES), jnp.float32),
-            pltpu.VMEM((2, 3, 2, 2, 2, UNIT, LANES), jnp.float32),
-            dma((3,)), dma((3, ITEMS)), dma((2, 3)),
+            pltpu.VMEM((2, 3, 2, 2, 2, GROUP, LANES), jnp.float32),
+            dma((3,)), dma((3, ITEMS // 2)), dma((2, 3)),
             dma((3, 3)), dma((3, 3, ITEMS)), dma((3,)), dma((3,)), dma((3,)),
         ],
         compiler_params=pltpu.CompilerParams(has_side_effects=True, vmem_limit_bytes=67043328),

time: 347 us -> 347 us (level)
  no operation moved by 1% of the time
where the time goes in v5:
time: 347 us
  Pallas kernels  343 us (99%)
    pallas_call x1, Pallas kernels, scatter(): pl.pallas_call(scatter_kernel, out_shape=(jax.ShapeDtypeStruct((WINDOW, L...  206 us
    pallas_call x1, Pallas kernels, gather(): pl.pallas_call(gather_kernel, out_shape=jax.ShapeDtypeStruct((2, 2, 2, 2,...  105 us
    pallas_call x1, Pallas kernels, mid(): pl.pallas_call(mid_kernel, out_shape=(shard, shard, shard, jax.ShapeDtype...  19.2 us
    pallas_call x1, Pallas kernels, finish(): pl.pallas_call(final_kernel, out_shape=tuple((shape(end - base) for base,...  12.3 us

profile of v5, /device:TPU:0, one launch (start us, length us, event | category | flops | bytes accessed | tf_op | source)
XLA Modules:
  0.0 346.9 jit_solution(5561721400841212554)
XLA Ops:
  0.6 0.9 reduce
  1.6 0.6 pad_bitcast_fusion.b_ref
  2.2 206.2 %shard_map.151 = (f32[7296,128]{1,0:T(8,128)}, f32[98304]{0:T(1024)}) custom-call(f32[32768,128]{1,0:T(8,128)} %bitcast.44, f32[32768,128]{1,0:T(8,128)} %bitcast.45, f32[22528,128]{1,0:T(8,128)} %bitcast.46, f32[22528,128]{1,0:T(8,128)} %bitcast.47, f32[128,128]{1,0:T(8,128)} %pad_bitcast_fusion.b_ref, f32[885488]{0:T(1024)} %m_ref.3, f32[885488]{0:T(1024)} %v_ref.3, ...), custom_call_target="tpu_custom_call" | custom-call | tf_op jit(solution)/shard_map/pallas_call | solution.py:260
  208.4 19.2 %shard_map.152 = (f32[885488]{0:T(1024)}, f32[885488]{0:T(1024)}, f32[885488]{0:T(1024)}, bf16[7104,128]{1,0:T(8,128)(2,1)}) custom-call(f32[7296,128]{1,0:T(8,128)} %get-tuple-element.21.tile_ref, f32[885488]{0:T(1024)} %m_ref.3, f32[885488]{0:T(1024)} %v_ref.3, f32[885488]{0:T(1024)} %w_ref.3, f32[98304]{0:T(1024)} %get-tuple-element.22.edge_ref), custom_call_target="tpu_custom_call" | custom-call | tf_op jit(solution)/shard_map/pallas_call | solution.py:511
  227.7 0.0 copy-start
  227.7 1.5 copy-done
  229.2 105.4 %shard_map.153 = bf16[2,2,2,2,7104,128]{5,4,3,2,1,0:T(8,128)(2,1)S(1)} custom-call(bf16[7104,128]{1,0:T(8,128)(2,1)S(1)} %copy-done), custom_call_target="tpu_custom_call" | custom-call | tf_op jit(solution)/shard_map/pallas_call | solution.py:355
  334.5 12.3 %shard_map.154 = (bf16[32768,128]{1,0:T(8,128)(2,1)}, bf16[32768,128]{1,0:T(8,128)(2,1)}, bf16[22528,128]{1,0:T(8,128)(2,1)}, bf16[22528,128]{1,0:T(8,128)(2,1)}...) custom-call(bf16[16,7104,128]{2,1,0:T(8,128)(2,1)S(1)} %bitcast.43), custom_call_target="tpu_custom_call" | custom-call | tf_op jit(solution)/shard_map/pallas_call | solution.py:628
Async XLA Ops:
  227.7 1.5 copy-start

commit v6 on v5

--- a/solution.py
+++ b/solution.py
@@ -22,8 +22,10 @@
 VEC_BLOCK_ROWS = 128
 UNIT = 64
 GROUP = 128
-WINDOW = 7296
-COUNTS = (38, 38, 38)
+COMMON = 7168
+WINDOW = COMMON + GROUP
+LONG_SLICE = 10
+COUNTS = (38, 38, 36)
 FIRSTS = (0, 38, 76)
 ITEMS = max(COUNTS)
 LAG = 2
@@ -50,7 +52,7 @@
 
 def window_start(index):
     row = floor_block(index * (SLICE // 16) // 8)
-    return jnp.minimum(row // GROUP * GROUP, ROWS - WINDOW)
+    return jnp.minimum(row // GROUP * GROUP, ROWS - COMMON)
 
 
 def own_start_static(index):
@@ -113,7 +115,7 @@
 
 def scatter_kernel(e_ref, a_ref, f_ref, h_ref, b_ref, m_ref, v_ref, w_ref, out_ref, edge_ref,
                    part, recv0, recv1, recv2, mine, pair_send, pair_recv, mine_sem,
-                   send, arrive, out_sem, edge_send, edge_recv):
+                   send, arrive, out_sem, edge_send, edge_recv, long_mine, long_part, long_recv, long_sem):
     z, y, x, core = position()
     chip = (z * 2 + y) * 2 + x
     device = chip * 2 + core
@@ -138,6 +140,15 @@
     def item_row(third, item):
         return pl.multiple_of((FIRSTS[third] + item) * UNIT, UNIT)
 
+    def each_third(index, counts, action):
+        for third in range(3):
+            if counts[third] == max(counts):
+                action(third)
+            else:
+                @pl.when(index < counts[third])
+                def _():
+                    action(third)
+
     def group_row(third, group):
         return pl.multiple_of(FIRSTS[third] * UNIT + group * GROUP, GROUP)
 
@@ -148,7 +159,8 @@
             other = ((z + jz) % 2 * 2 + (y + jy) % 2) * 2 + (x + jx) % 2
             theirs = window_start(other * 2 + 1 - core)
             ours = window_start(other * 2 + core)
-            for third in range(3):
+
+            def action(third):
                 row = group_row(third, group)
                 from_source(theirs + row, lambda src: pltpu.make_async_remote_copy(
                     src_ref=src, dst_ref=part.at[jz, jy, jx, pl.ds(row, GROUP), :],
@@ -156,6 +168,7 @@
                     device_id=neighbour(3), device_id_type=MESH).start())
                 from_source(ours + row, lambda src: pltpu.make_async_copy(
                     src, mine.at[slot, third, jz, jy, jx], mine_sem.at[slot, third]).start())
+            each_third(group, [count // 2 for count in COUNTS], action)
 
     def hop_copy(third, item, hop, whole=False):
         rows = pl.ds(item_row(third, 0), COUNTS[third] * UNIT) if whole else pl.ds(item_row(third, item), UNIT)
@@ -226,6 +239,78 @@
         hop_copy(third, item, 2).wait_recv()
         part[0, 0, 0, rows, :] = (part[0, 0, 0, rows, :] + recv2[rows, :]) / SIXTEEN
 
+    long_chip, long_core = LONG_SLICE // 2, LONG_SLICE % 2
+    lz, ly, lx = (z + long_chip // 4) % 2, (y + long_chip // 2 % 2) % 2, (x + long_chip % 2) % 2
+    long_row = window_start(LONG_SLICE) + COMMON
+    holder = core == long_core
+
+    def long_pair():
+        return pltpu.make_async_remote_copy(
+            src_ref=long_mine, dst_ref=long_part, send_sem=long_sem.at[0], recv_sem=long_sem.at[1],
+            device_id=neighbour(3), device_id_type=MESH)
+
+    def long_load():
+        return pltpu.make_async_copy(
+            sources[2].at[pl.ds(pl.multiple_of(long_row - TENSORS[2][0], GROUP), GROUP), :], long_mine, long_sem.at[2])
+
+    def long_hop(hop):
+        return pltpu.make_async_remote_copy(
+            src_ref=long_part, dst_ref=long_recv.at[hop], send_sem=long_sem.at[3 + hop], recv_sem=long_sem.at[6 + hop],
+            device_id=neighbour((2, 0, 1)[hop]), device_id_type=MESH)
+
+    def long_out():
+        return pltpu.make_async_copy(long_part, out_ref.at[pl.ds(COMMON, GROUP), :], long_sem.at[9])
+
+    reached = (holder, holder & (lx == 0), holder & (lx == 0) & (lz == 0), holder & (lx == 0) & (lz == 0) & (ly == 0))
+    far = (lx == 1, lz == 1, ly == 1)
+
+    def long_start():
+        long_load().start()
+
+    def long_exchange():
+        long_load().wait()
+
+        @pl.when(core != long_core)
+        def _():
+            long_pair().start()
+
+    def long_sum():
+        @pl.when(holder)
+        def _():
+            long_pair().wait_recv()
+            long_part[...] += long_mine[...]
+
+        @pl.when(core != long_core)
+        def _():
+            long_pair().wait_send()
+
+    def long_send(hop):
+        @pl.when(reached[hop] & far[hop])
+        def _():
+            long_hop(hop).start()
+
+    def long_add(hop):
+        @pl.when(reached[hop] & far[hop])
+        def _():
+            long_hop(hop).wait_send()
+
+        @pl.when(reached[hop + 1])
+        def _():
+            long_hop(hop).wait_recv()
+            if hop < 2:
+                long_part[...] += long_recv[hop]
+            else:
+                long_part[...] = (long_part[...] + long_recv[hop]) / SIXTEEN
+
+    def long_store():
+        @pl.when(reached[3])
+        def _():
+            long_out().start()
+
+    long_stages = ((4, long_start), (6, long_exchange), (8, long_sum)) + tuple(
+        (9 + 3 * hop + k, functools.partial((long_send, long_add)[k // 2], hop)) for hop in range(3) for k in (0, 2)
+    ) + ((19, long_store),)
+
     stages = ((0, stage0), (LAG, stage1), (2 * LAG, stage2), (3 * LAG, stage3),
               (3 * LAG + 1, lambda item, third: out_copy(third, item).start()))
 
@@ -234,8 +319,12 @@
         for delay, stage in stages:
             @pl.when((step >= delay) & (step < ITEMS + delay))
             def _():
-                for third in range(3):
-                    stage(step - delay, third)
+                each_third(step - delay, COUNTS, functools.partial(stage, step - delay))
+
+        for at, stage in long_stages:
+            @pl.when(step == at)
+            def _():
+                stage()
 
         @pl.when((step % 2 == 0) & (step + 2 < ITEMS))
         def _():
@@ -246,6 +335,10 @@
         for hop in range(3):
             hop_copy(third, 0, hop, True).wait_send()
         out_copy(third, 0, True).wait()
+
+    @pl.when(reached[3])
+    def _():
+        long_out().wait()
 
     for n, ref in enumerate((m_ref, v_ref, w_ref)):
         pltpu.make_async_remote_copy(
@@ -263,13 +356,15 @@
         in_specs=[any_spec] * 8,
         out_specs=(any_spec, any_spec),
         scratch_shapes=[
-            pltpu.VMEM((2, 2, 2, WINDOW, LANES), jnp.float32),
-            pltpu.VMEM((2, 2, WINDOW, LANES), jnp.float32),
-            pltpu.VMEM((2, WINDOW, LANES), jnp.float32),
-            pltpu.VMEM((WINDOW, LANES), jnp.float32),
+            pltpu.VMEM((2, 2, 2, COMMON, LANES), jnp.float32),
+            pltpu.VMEM((2, 2, COMMON, LANES), jnp.float32),
+            pltpu.VMEM((2, COMMON, LANES), jnp.float32),
+            pltpu.VMEM((COMMON, LANES), jnp.float32),
             pltpu.VMEM((2, 3, 2, 2, 2, GROUP, LANES), jnp.float32),
             dma((3,)), dma((3, ITEMS // 2)), dma((2, 3)),
             dma((3, 3)), dma((3, 3, ITEMS)), dma((3,)), dma((3,)), dma((3,)),
+            pltpu.VMEM((GROUP, LANES), jnp.float32), pltpu.VMEM((GROUP, LANES), jnp.float32),
+            pltpu.VMEM((3, GROUP, LANES), jnp.float32), dma((10,)),
         ],
         compiler_params=pltpu.CompilerParams(has_side_effects=True, vmem_limit_bytes=67043328),
     )(*grads, m, v, w)
@@ -375,9 +470,18 @@
         low = (jnp.maximum(start, base) - base + block - 1) // block
         high = jnp.maximum(jnp.minimum(start + length, end) - base, 0) // block
 
-        @pl.loop(low, jnp.maximum(high, low))
+        count = jnp.maximum(high - low, 0)
+        together = 4 if tiles <= 8 else 1
+
+        @pl.loop(0, count // together)
         def _(n):
-            action(pl.multiple_of(base + n * block - start, 8), tiles)
+            for k in range(together):
+                action(pl.multiple_of(base + (low + n * together + k) * block - start, 8), tiles)
+
+        if together > 1:
+            @pl.loop(count // together * together, count)
+            def _(n):
+                action(pl.multiple_of(base + (low + n) * block - start, 8), tiles)
 
 
 PAD = 8
@@ -393,9 +497,9 @@
     return lax.broadcasted_iota(jnp.int32, (rows, LANES), 1)
 
 
-BATCH = 128
+BATCH = 256
 BATCHES = SHARD_VREGS * 8 // BATCH
-CHUNK_BATCHES = 6
+CHUNK_BATCHES = 3
 CHUNKS = BATCHES // CHUNK_BATCHES
 CHUNK = CHUNK_BATCHES * BATCH * LANES
 
@@ -644,7 +748,7 @@
     def local_step(g_embed, g_attn, g_ffn_in, g_ffn_out, g_vec, m_shard, v_shard, w_shard):
         matrices = (g_embed, g_attn, g_ffn_in, g_ffn_out)
         grads = [to_tiles(g[0] if g.ndim == 3 else g[0, 0]) for g in matrices]
-        grads.append(jnp.pad(g_vec.reshape(-1), (0, VEC_BLOCK_ROWS * LANES - VEC_WIDTH)).reshape(VEC_BLOCK_ROWS, LANES))
+        grads.append(jnp.pad(g_vec, ((0, 0), (0, 0), (0, VEC_BLOCK_ROWS * LANES - VEC_WIDTH))).reshape(VEC_BLOCK_ROWS, LANES))
         mean_tiles, edges = scatter(grads, m_shard, v_shard, w_shard)
         m_new, v_new, w_new, w_own = mid(mean_tiles, m_shard, v_shard, w_shard, edges)
         full = gather(w_own).reshape(SIXTEEN, OWN, LANES)

time: 347 us -> 344 us (level)
    pallas_call x1, Pallas kernels: 19.2 us -> 15.3 us  [mid(): pl.pallas_call(mid_kernel, out_shape=(shard, shard, shard, jax.ShapeDtype...]
where the time goes in v6:
time: 344 us; the launch traced here: 343 us
  Pallas kernels  340 us (99%)
    pallas_call x1, Pallas kernels, scatter(): pl.pallas_call(scatter_kernel, out_shape=(jax.ShapeDtypeStruct((WINDOW, L...  206 us
    pallas_call x1, Pallas kernels, gather(): pl.pallas_call(gather_kernel, out_shape=jax.ShapeDtypeStruct((2, 2, 2, 2,...  106 us
    pallas_call x1, Pallas kernels, mid(): pl.pallas_call(mid_kernel, out_shape=(shard, shard, shard, jax.ShapeDtype...  15.3 us
    pallas_call x1, Pallas kernels, finish(): pl.pallas_call(final_kernel, out_shape=tuple((shape(end - base) for base,...  12.3 us

profile of v6, /device:TPU:0, one launch (start us, length us, event | category | flops | bytes accessed | tf_op | source)
XLA Modules:
  0.0 343.3 jit_solution(3881297101148457872)
XLA Ops:
  0.6 1.5 pad.4
  2.1 206.0 %shard_map.151 = (f32[7296,128]{1,0:T(8,128)}, f32[98304]{0:T(1024)}) custom-call(f32[32768,128]{1,0:T(8,128)} %bitcast.43, f32[32768,128]{1,0:T(8,128)} %bitcast.44, f32[22528,128]{1,0:T(8,128)} %bitcast.45, f32[22528,128]{1,0:T(8,128)} %bitcast.46, f32[128,128]{1,0:T(8,128)} %bitcast.47, f32[885488]{0:T(1024)} %m_ref.3, f32[885488]{0:T(1024)} %v_ref.3, ...), custom_call_target="tpu_custom_call" | custom-call | tf_op jit(solution)/shard_map/pallas_call | solution.py:353
  208.1 15.3 %shard_map.152 = (f32[885488]{0:T(1024)}, f32[885488]{0:T(1024)}, f32[885488]{0:T(1024)}, bf16[7104,128]{1,0:T(8,128)(2,1)}) custom-call(f32[7296,128]{1,0:T(8,128)} %get-tuple-element.21.tile_ref, f32[885488]{0:T(1024)} %m_ref.3, f32[885488]{0:T(1024)} %v_ref.3, f32[885488]{0:T(1024)} %w_ref.3, f32[98304]{0:T(1024)} %get-tuple-element.22.edge_ref), custom_call_target="tpu_custom_call" | custom-call | tf_op jit(solution)/shard_map/pallas_call | solution.py:615
  223.4 0.0 copy-start
  223.4 1.5 copy-done
  224.9 106.1 %shard_map.153 = bf16[2,2,2,2,7104,128]{5,4,3,2,1,0:T(8,128)(2,1)S(1)} custom-call(bf16[7104,128]{1,0:T(8,128)(2,1)S(1)} %copy-done), custom_call_target="tpu_custom_call" | custom-call | tf_op jit(solution)/shard_map/pallas_call | solution.py:450
  331.0 12.3 %shard_map.154 = (bf16[32768,128]{1,0:T(8,128)(2,1)}, bf16[32768,128]{1,0:T(8,128)(2,1)}, bf16[22528,128]{1,0:T(8,128)(2,1)}, bf16[22528,128]{1,0:T(8,128)(2,1)}...) custom-call(bf16[16,7104,128]{2,1,0:T(8,128)(2,1)S(1)} %bitcast.42), custom_call_target="tpu_custom_call" | custom-call | tf_op jit(solution)/shard_map/pallas_call | solution.py:732
Async XLA Ops:
  223.4 1.5 copy-start

commit v7 on v6

--- a/solution.py
+++ b/solution.py
@@ -38,7 +38,7 @@
 SIXTEEN = 16
 FINAL_LIMIT = 20000000
 GATHER_LIMIT = 6000000
-MID_LIMIT = 64000000
+MID_LIMIT = 52000000
 
 
 def floor_block(row):
@@ -113,6 +113,13 @@
     return (z, y, 2 * x + core)
 
 
+def meet(devices):
+    barrier = pltpu.get_barrier_semaphore()
+    for device in devices:
+        pl.semaphore_signal(barrier, inc=1, device_id=device, device_id_type=MESH)
+    pl.semaphore_wait(barrier, len(devices))
+
+
 def scatter_kernel(e_ref, a_ref, f_ref, h_ref, b_ref, m_ref, v_ref, w_ref, out_ref, edge_ref,
                    part, recv0, recv1, recv2, mine, pair_send, pair_recv, mine_sem,
                    send, arrive, out_sem, edge_send, edge_recv, long_mine, long_part, long_recv, long_sem):
@@ -122,6 +129,8 @@
     sources = (e_ref, a_ref, f_ref, h_ref, b_ref)
 
     before = (device + SIXTEEN - 1) % SIXTEEN
+    after = (device + 1) % SIXTEEN
+    meet([neighbour(axis) for axis in range(4)] + [(d // 8, d // 4 % 2, d % 4) for d in (before, after)])
     for n, ref in enumerate((m_ref, v_ref, w_ref)):
         pltpu.make_async_remote_copy(
             src_ref=ref.at[pl.ds(0, EDGE)], dst_ref=edge_ref.at[pl.ds(n * EDGE, EDGE)],
@@ -366,7 +375,7 @@
             pltpu.VMEM((GROUP, LANES), jnp.float32), pltpu.VMEM((GROUP, LANES), jnp.float32),
             pltpu.VMEM((3, GROUP, LANES), jnp.float32), dma((10,)),
         ],
-        compiler_params=pltpu.CompilerParams(has_side_effects=True, vmem_limit_bytes=67043328),
+        compiler_params=pltpu.CompilerParams(has_side_effects=True, collective_id=0, vmem_limit_bytes=67043328),
     )(*grads, m, v, w)
 
 
@@ -406,6 +415,7 @@
             src_ref=block, dst_ref=block, send_sem=pair_send.at[third], recv_sem=pair_recv.at[third, item],
             device_id=neighbour(3), device_id_type=MESH)
 
+    meet([neighbour(axis) for axis in range(4)])
     for item in range(OWN_LAG):
         for third in range(3):
             copy(third, item, 0).start()
@@ -455,7 +465,7 @@
         scratch_shapes=[
             dma((3,)), dma((3, OWN_ITEMS)), dma((3, 3)), dma((3, OWN_ITEMS, 3)),
         ],
-        compiler_params=pltpu.CompilerParams(has_side_effects=True, vmem_limit_bytes=GATHER_LIMIT),
+        compiler_params=pltpu.CompilerParams(has_side_effects=True, collective_id=1, vmem_limit_bytes=GATHER_LIMIT),
     )(w_own)
 
 

time: 344 us -> 337 us (0.980)
  Pallas kernels: 340 us -> 333 us
where the time goes in v7:
time: 337 us; the launch traced here: 336 us
  Pallas kernels  333 us (99%)
    pallas_call x1, Pallas kernels, scatter(): pl.pallas_call(scatter_kernel, out_shape=(jax.ShapeDtypeStruct((WINDOW, L...  204 us
    pallas_call x1, Pallas kernels, gather(): pl.pallas_call(gather_kernel, out_shape=jax.ShapeDtypeStruct((2, 2, 2, 2,...  103 us
    pallas_call x1, Pallas kernels, mid(): pl.pallas_call(mid_kernel, out_shape=(shard, shard, shard, jax.ShapeDtype...  14 us
    pallas_call x1, Pallas kernels, finish(): pl.pallas_call(final_kernel, out_shape=tuple((shape(end - base) for base,...  12.3 us

profile of v7, /device:TPU:0, one launch (start us, length us, event | category | flops | bytes accessed | tf_op | source)
XLA Modules:
  0.0 336.5 jit_solution(1150850255456985822)
XLA Ops:
  0.6 1.5 pad.4
  2.1 203.6 %shard_map.151 = (f32[7296,128]{1,0:T(8,128)}, f32[98304]{0:T(1024)}) custom-call(f32[32768,128]{1,0:T(8,128)} %bitcast.43, f32[32768,128]{1,0:T(8,128)} %bitcast.44, f32[22528,128]{1,0:T(8,128)} %bitcast.45, f32[22528,128]{1,0:T(8,128)} %bitcast.46, f32[128,128]{1,0:T(8,128)} %bitcast.47, f32[885488]{0:T(1024)} %m_ref.3, f32[885488]{0:T(1024)} %v_ref.3, ...), custom_call_target="tpu_custom_call" | custom-call | tf_op jit(solution)/shard_map/pallas_call | solution.py:362
  205.7 0.0 copy-start
  205.7 1.0 copy-done
  206.7 14.0 %shard_map.152 = (f32[885488]{0:T(1024)}, f32[885488]{0:T(1024)}, f32[885488]{0:T(1024)}, bf16[7104,128]{1,0:T(8,128)(2,1)S(1)}) custom-call(f32[7296,128]{1,0:T(8,128)} %get-tuple-element.21.tile_ref, f32[885488]{0:T(1024)} %m_ref.3, f32[885488]{0:T(1024)} %v_ref.3, f32[885488]{0:T(1024)} %w_ref.3, f32[98304]{0:T(1024)S(1)} %copy-done), custom_call_target="tpu_custom_call" | custom-call | tf_op jit(solution)/shard_map/pallas_call | solution.py:625
  220.7 103.4 %shard_map.153 = bf16[2,2,2,2,7104,128]{5,4,3,2,1,0:T(8,128)(2,1)S(1)} custom-call(bf16[7104,128]{1,0:T(8,128)(2,1)S(1)} %get-tuple-element.26.w_ref), custom_call_target="tpu_custom_call" | custom-call | tf_op jit(solution)/shard_map/pallas_call | solution.py:460
  324.1 12.3 %shard_map.154 = (bf16[32768,128]{1,0:T(8,128)(2,1)}, bf16[32768,128]{1,0:T(8,128)(2,1)}, bf16[22528,128]{1,0:T(8,128)(2,1)}, bf16[22528,128]{1,0:T(8,128)(2,1)}...) custom-call(bf16[16,7104,128]{2,1,0:T(8,128)(2,1)S(1)} %bitcast.42), custom_call_target="tpu_custom_call" | custom-call | tf_op jit(solution)/shard_map/pallas_call | solution.py:742
Async XLA Ops:
  205.7 1.0 copy-start

commit v8 on v7

--- a/solution.py
+++ b/solution.py
@@ -122,11 +122,13 @@
 
 def scatter_kernel(e_ref, a_ref, f_ref, h_ref, b_ref, m_ref, v_ref, w_ref, out_ref, edge_ref,
                    part, recv0, recv1, recv2, mine, pair_send, pair_recv, mine_sem,
-                   send, arrive, out_sem, edge_send, edge_recv, long_mine, long_part, long_recv, long_sem):
+                   send, arrive, out_sem, edge_send, edge_recv, long_mine, long_part, long_recv, long_sem, vec_raw, vec_rows, vec_sem):
     z, y, x, core = position()
     chip = (z * 2 + y) * 2 + x
     device = chip * 2 + core
-    sources = (e_ref, a_ref, f_ref, h_ref, b_ref)
+    sources = (e_ref, a_ref, f_ref, h_ref, vec_rows)
+    vec_load = pltpu.make_async_copy(b_ref, vec_raw, vec_sem)
+    vec_load.start()
 
     before = (device + SIXTEEN - 1) % SIXTEEN
     after = (device + 1) % SIXTEEN
@@ -161,22 +163,23 @@
     def group_row(third, group):
         return pl.multiple_of(FIRSTS[third] * UNIT + group * GROUP, GROUP)
 
-    def start_group(group, slot):
-        @pl.loop(0, 8)
-        def _(j):
-            jz, jy, jx = j // 4, j // 2 % 2, j % 2
-            other = ((z + jz) % 2 * 2 + (y + jy) % 2) * 2 + (x + jx) % 2
-            theirs = window_start(other * 2 + 1 - core)
-            ours = window_start(other * 2 + core)
-
+    def start_group(group, slot, side):
+        @pl.loop(0, 4)
+        def _(n):
             def action(third):
+                index = [n // 2, n % 2]
+                index = index[:ORDERS[third][0]] + [side] + index[ORDERS[third][0]:]
+                jz, jy, jx = index
+                other = ((z + jz) % 2 * 2 + (y + jy) % 2) * 2 + (x + jx) % 2
+                theirs = window_start(other * 2 + 1 - core)
+                ours = window_start(other * 2 + core)
                 row = group_row(third, group)
                 from_source(theirs + row, lambda src: pltpu.make_async_remote_copy(
                     src_ref=src, dst_ref=part.at[jz, jy, jx, pl.ds(row, GROUP), :],
-                    send_sem=pair_send.at[third], recv_sem=pair_recv.at[third, group],
+                    send_sem=pair_send.at[third], recv_sem=pair_recv.at[side, third, group],
                     device_id=neighbour(3), device_id_type=MESH).start())
                 from_source(ours + row, lambda src: pltpu.make_async_copy(
-                    src, mine.at[slot, third, jz, jy, jx], mine_sem.at[slot, third]).start())
+                    src, mine.at[slot, third, side, n], mine_sem.at[slot, third, side]).start())
             each_third(group, [count // 2 for count in COUNTS], action)
 
     def hop_copy(third, item, hop, whole=False):
@@ -196,33 +199,44 @@
             send_sem=send.at[third, hop], recv_sem=arrive.at[third, hop, item],
             device_id=neighbour(ORDERS[third][hop]), device_id_type=MESH)
 
-    def pair_all(third, group, whole=False):
-        rows = pl.ds(FIRSTS[third] * UNIT, COUNTS[third] * UNIT) if whole else pl.ds(group_row(third, group), GROUP)
-        block = part.at[:, :, :, rows, :]
+    def pair_side(third, group, side):
+        index = tuple(side if n == ORDERS[third][0] else slice(None) for n in range(3))
+        block = part.at[index + (pl.ds(group_row(third, group), GROUP), slice(None))]
         return pltpu.make_async_remote_copy(
-            src_ref=block, dst_ref=block, send_sem=pair_send.at[third], recv_sem=pair_recv.at[third, group],
+            src_ref=block, dst_ref=block, send_sem=pair_send.at[third], recv_sem=pair_recv.at[side, third, group],
+            device_id=neighbour(3), device_id_type=MESH)
+
+    def pair_whole(third):
+        block = part.at[:, :, :, pl.ds(FIRSTS[third] * UNIT, COUNTS[third] * UNIT), :]
+        return pltpu.make_async_remote_copy(
+            src_ref=block, dst_ref=block, send_sem=pair_send.at[third], recv_sem=pair_recv.at[0, third, 0],
             device_id=neighbour(3), device_id_type=MESH)
 
     def out_copy(third, item, whole=False):
         rows = pl.ds(item_row(third, 0), COUNTS[third] * UNIT) if whole else pl.ds(item_row(third, item), UNIT)
         return pltpu.make_async_copy(part.at[0, 0, 0, rows, :], out_ref.at[rows, :], out_sem.at[third])
 
-    start_group(0, 0)
-
-    def stage0(item, third):
+    start_group(0, 0, 1)
+    start_group(0, 0, 0)
+
+    def add_mine(side, item, third):
         rows = pl.ds(item_row(third, item), UNIT)
         group = item // 2
         slot = group % 2
 
         @pl.when(item % 2 == 0)
         def _():
-            pltpu.make_async_copy(mine.at[slot, third], mine.at[slot, third], mine_sem.at[slot, third]).wait()
-            pair_all(third, group).wait_recv()
+            block = mine.at[slot, third, side]
+            pltpu.make_async_copy(block, block, mine_sem.at[slot, third, side]).wait()
+            pair_side(third, group, side).wait_recv()
         within = pl.ds(pl.multiple_of(item % 2 * UNIT, UNIT), UNIT)
-        for j in range(8):
-            index = (j // 4, j // 2 % 2, j % 2)
-            part[index + (rows, slice(None))] += mine[(slot, third) + index + (within, slice(None))]
-        hop_copy(third, item, 0).start()
+        first = ORDERS[third][0]
+        for n in range(4):
+            index = [n // 2, n % 2]
+            index = tuple(index[:first] + [side] + index[first:])
+            part[index + (rows, slice(None))] += mine[slot, third, side, n, within, :]
+        if side:
+            hop_copy(third, item, 0).start()
 
     def stage1(item, third):
         rows = pl.ds(item_row(third, item), UNIT)
@@ -320,8 +334,15 @@
         (9 + 3 * hop + k, functools.partial((long_send, long_add)[k // 2], hop)) for hop in range(3) for k in (0, 2)
     ) + ((19, long_store),)
 
-    stages = ((0, stage0), (LAG, stage1), (2 * LAG, stage2), (3 * LAG, stage3),
+    stages = ((0, functools.partial(add_mine, 1)), (0, functools.partial(add_mine, 0)), (LAG, stage1), (2 * LAG, stage2), (3 * LAG, stage3),
               (3 * LAG + 1, lambda item, third: out_copy(third, item).start()))
+
+    vec_load.wait()
+    vec_rows[pl.ds(VEC_ROWS // 8 * 8, VEC_BLOCK_ROWS - VEC_ROWS // 8 * 8), :] = jnp.zeros(
+        (VEC_BLOCK_ROWS - VEC_ROWS // 8 * 8, LANES), jnp.float32)
+    for n in range(-(-VEC_ROWS // 8)):
+        rows = min(8, VEC_ROWS - n * 8)
+        vec_rows[n * 8:n * 8 + rows, :] = vec_raw[:, n * 1024:n * 1024 + rows * LANES].reshape(rows, LANES)
 
     @pl.loop(0, ITEMS + stages[-1][0])
     def _(step):
@@ -337,10 +358,11 @@
 
         @pl.when((step % 2 == 0) & (step + 2 < ITEMS))
         def _():
-            start_group(step // 2 + 1, (step // 2 + 1) % 2)
+            start_group(step // 2 + 1, (step // 2 + 1) % 2, 1)
+            start_group(step // 2 + 1, (step // 2 + 1) % 2, 0)
 
     for third in range(3):
-        pair_all(third, 0, True).wait_send()
+        pair_whole(third).wait_send()
         for hop in range(3):
             hop_copy(third, 0, hop, True).wait_send()
         out_copy(third, 0, True).wait()
@@ -369,11 +391,12 @@
             pltpu.VMEM((2, 2, COMMON, LANES), jnp.float32),
             pltpu.VMEM((2, COMMON, LANES), jnp.float32),
             pltpu.VMEM((COMMON, LANES), jnp.float32),
-            pltpu.VMEM((2, 3, 2, 2, 2, GROUP, LANES), jnp.float32),
-            dma((3,)), dma((3, ITEMS // 2)), dma((2, 3)),
+            pltpu.VMEM((2, 3, 2, 4, GROUP, LANES), jnp.float32),
+            dma((3,)), dma((2, 3, ITEMS // 2)), dma((2, 3, 2)),
             dma((3, 3)), dma((3, 3, ITEMS)), dma((3,)), dma((3,)), dma((3,)),
             pltpu.VMEM((GROUP, LANES), jnp.float32), pltpu.VMEM((GROUP, LANES), jnp.float32),
             pltpu.VMEM((3, GROUP, LANES), jnp.float32), dma((10,)),
+            pltpu.VMEM((1, VEC_WIDTH), jnp.float32), pltpu.VMEM((VEC_BLOCK_ROWS, LANES), jnp.float32), dma(()),
         ],
         compiler_params=pltpu.CompilerParams(has_side_effects=True, collective_id=0, vmem_limit_bytes=67043328),
     )(*grads, m, v, w)
@@ -758,7 +781,7 @@
     def local_step(g_embed, g_attn, g_ffn_in, g_ffn_out, g_vec, m_shard, v_shard, w_shard):
         matrices = (g_embed, g_attn, g_ffn_in, g_ffn_out)
         grads = [to_tiles(g[0] if g.ndim == 3 else g[0, 0]) for g in matrices]
-        grads.append(jnp.pad(g_vec, ((0, 0), (0, 0), (0, VEC_BLOCK_ROWS * LANES - VEC_WIDTH))).reshape(VEC_BLOCK_ROWS, LANES))
+        grads.append(g_vec.reshape(1, -1))
         mean_tiles, edges = scatter(grads, m_shard, v_shard, w_shard)
         m_new, v_new, w_new, w_own = mid(mean_tiles, m_shard, v_shard, w_shard, edges)
         full = gather(w_own).reshape(SIXTEEN, OWN, LANES)

time: 337 us -> 336 us (level)
  no operation moved by 1% of the time
where the time goes in v8:
time: 336 us
  Pallas kernels  334 us (99%)
    pallas_call x1, Pallas kernels, scatter(): pl.pallas_call(scatter_kernel, out_shape=(jax.ShapeDtypeStruct((WINDOW, L...  204 us
    pallas_call x1, Pallas kernels, gather(): pl.pallas_call(gather_kernel, out_shape=jax.ShapeDtypeStruct((2, 2, 2, 2,...  103 us
    pallas_call x1, Pallas kernels, mid(): pl.pallas_call(mid_kernel, out_shape=(shard, shard, shard, jax.ShapeDtype...  14 us
    pallas_call x1, Pallas kernels, finish(): pl.pallas_call(final_kernel, out_shape=tuple((shape(end - base) for base,...  12.3 us

profile of v8, /device:TPU:0, one launch (start us, length us, event | category | flops | bytes accessed | tf_op | source)
XLA Modules:
  0.0 335.8 jit_solution(12046808002759339827)
XLA Ops:
  0.6 204.4 %shard_map.151 = (f32[7296,128]{1,0:T(8,128)}, f32[98304]{0:T(1024)}) custom-call(f32[32768,128]{1,0:T(8,128)} %bitcast.43, f32[32768,128]{1,0:T(8,128)} %bitcast.44, f32[22528,128]{1,0:T(8,128)} %bitcast.45, f32[22528,128]{1,0:T(8,128)} %bitcast.46, f32[1,12032]{1,0:T(1,128)} %bitcast.47, f32[885488]{0:T(1024)} %m_ref.3, f32[885488]{0:T(1024)} %v_ref.3, ...), custom_call_target="tpu_custom_call" | custom-call | tf_op jit(solution)/shard_map/pallas_call | solution.py:384
  205.0 0.0 copy-start
  205.0 1.0 copy-done
  206.0 14.0 %shard_map.152 = (f32[885488]{0:T(1024)}, f32[885488]{0:T(1024)}, f32[885488]{0:T(1024)}, bf16[7104,128]{1,0:T(8,128)(2,1)S(1)}) custom-call(f32[7296,128]{1,0:T(8,128)} %get-tuple-element.21.tile_ref, f32[885488]{0:T(1024)} %m_ref.3, f32[885488]{0:T(1024)} %v_ref.3, f32[885488]{0:T(1024)} %w_ref.3, f32[98304]{0:T(1024)S(1)} %copy-done), custom_call_target="tpu_custom_call" | custom-call | tf_op jit(solution)/shard_map/pallas_call | solution.py:648
  220.0 103.4 %shard_map.153 = bf16[2,2,2,2,7104,128]{5,4,3,2,1,0:T(8,128)(2,1)S(1)} custom-call(bf16[7104,128]{1,0:T(8,128)(2,1)S(1)} %get-tuple-element.26.w_ref), custom_call_target="tpu_custom_call" | custom-call | tf_op jit(solution)/shard_map/pallas_call | solution.py:483
  323.5 12.3 %shard_map.154 = (bf16[32768,128]{1,0:T(8,128)(2,1)}, bf16[32768,128]{1,0:T(8,128)(2,1)}, bf16[22528,128]{1,0:T(8,128)(2,1)}, bf16[22528,128]{1,0:T(8,128)(2,1)}...) custom-call(bf16[16,7104,128]{2,1,0:T(8,128)(2,1)S(1)} %bitcast.42), custom_call_target="tpu_custom_call" | custom-call | tf_op jit(solution)/shard_map/pallas_call | solution.py:765
Async XLA Ops:
  205.0 1.0 copy-start

commit v9 on v7

--- a/solution.py
+++ b/solution.py
@@ -122,11 +122,13 @@
 
 def scatter_kernel(e_ref, a_ref, f_ref, h_ref, b_ref, m_ref, v_ref, w_ref, out_ref, edge_ref,
                    part, recv0, recv1, recv2, mine, pair_send, pair_recv, mine_sem,
-                   send, arrive, out_sem, edge_send, edge_recv, long_mine, long_part, long_recv, long_sem):
+                   send, arrive, out_sem, edge_send, edge_recv, long_mine, long_part, long_recv, long_sem, vec_raw, vec_rows, vec_sem):
     z, y, x, core = position()
     chip = (z * 2 + y) * 2 + x
     device = chip * 2 + core
-    sources = (e_ref, a_ref, f_ref, h_ref, b_ref)
+    sources = (e_ref, a_ref, f_ref, h_ref, vec_rows)
+    vec_load = pltpu.make_async_copy(b_ref, vec_raw, vec_sem)
+    vec_load.start()
 
     before = (device + SIXTEEN - 1) % SIXTEEN
     after = (device + 1) % SIXTEEN
@@ -322,6 +324,13 @@
 
     stages = ((0, stage0), (LAG, stage1), (2 * LAG, stage2), (3 * LAG, stage3),
               (3 * LAG + 1, lambda item, third: out_copy(third, item).start()))
+
+    vec_load.wait()
+    vec_rows[pl.ds(VEC_ROWS // 8 * 8, VEC_BLOCK_ROWS - VEC_ROWS // 8 * 8), :] = jnp.zeros(
+        (VEC_BLOCK_ROWS - VEC_ROWS // 8 * 8, LANES), jnp.float32)
+    for n in range(-(-VEC_ROWS // 8)):
+        rows = min(8, VEC_ROWS - n * 8)
+        vec_rows[n * 8:n * 8 + rows, :] = vec_raw[:, n * 1024:n * 1024 + rows * LANES].reshape(rows, LANES)
 
     @pl.loop(0, ITEMS + stages[-1][0])
     def _(step):
@@ -374,6 +383,7 @@
             dma((3, 3)), dma((3, 3, ITEMS)), dma((3,)), dma((3,)), dma((3,)),
             pltpu.VMEM((GROUP, LANES), jnp.float32), pltpu.VMEM((GROUP, LANES), jnp.float32),
             pltpu.VMEM((3, GROUP, LANES), jnp.float32), dma((10,)),
+            pltpu.VMEM((1, VEC_WIDTH), jnp.float32), pltpu.VMEM((VEC_BLOCK_ROWS, LANES), jnp.float32), dma(()),
         ],
         compiler_params=pltpu.CompilerParams(has_side_effects=True, collective_id=0, vmem_limit_bytes=67043328),
     )(*grads, m, v, w)
@@ -385,8 +395,13 @@
 
     def rows_of(third, item, whole=False):
         if whole:
-            return pl.ds(third * OWN_THIRD, OWN_THIRD)
-        return pl.ds(pl.multiple_of(third * OWN_THIRD + item * OWN_CHUNK, OWN_CHUNK), OWN_CHUNK)
+            return pl.ds(0, whole * OWN_CHUNK)
+        main = OWN_ITEMS - 1
+        row = jnp.where(item < main, third * main + item, 3 * main + third) * OWN_CHUNK
+        return pl.ds(pl.multiple_of(row, OWN_CHUNK), OWN_CHUNK)
+
+    def sent(item, side):
+        return (item < OWN_ITEMS - 1) | (side == 0)
 
     def copy(third, item, hop, whole=False):
         rows = rows_of(third, item, whole)
@@ -427,7 +442,7 @@
 
     @pl.loop(0, OWN_ITEMS + 2 * OWN_LAG)
     def _(step):
-        @pl.when(step + OWN_LAG < OWN_ITEMS)
+        @pl.when((step + OWN_LAG < OWN_ITEMS) & sent(step + OWN_LAG, core))
         def _():
             for third in range(3):
                 copy(third, step + OWN_LAG, 0).start()
@@ -435,7 +450,7 @@
         for hop in range(1, 4):
             delay = (hop - 1) * OWN_LAG
 
-            @pl.when((step >= delay) & (step < OWN_ITEMS + delay))
+            @pl.when((step >= delay) & (step < OWN_ITEMS + delay) & sent(step - delay, core))
             def _():
                 item = step - delay
                 for third in range(3):
@@ -447,12 +462,24 @@
 
     @pl.loop(0, OWN_ITEMS)
     def _(item):
+        @pl.when(sent(item, 1 - core))
+        def _():
+            for third in range(3):
+                pair(third, item, 1 - core).wait_recv()
+
+    def drain(count):
         for third in range(3):
-            pair(third, item, 1 - core).wait_recv()
-    for third in range(3):
-        pair(third, 0, core, True).wait_send()
-        for hop in range(3):
-            copy(third, 0, hop, True).wait_send()
+            pair(third, 0, core, count).wait_send()
+            for hop in range(3):
+                copy(third, 0, hop, count).wait_send()
+
+    @pl.when(core == 0)
+    def _():
+        drain(OWN_ITEMS)
+
+    @pl.when(core != 0)
+    def _():
+        drain(OWN_ITEMS - 1)
 
 
 def gather(w_own):
@@ -758,7 +785,7 @@
     def local_step(g_embed, g_attn, g_ffn_in, g_ffn_out, g_vec, m_shard, v_shard, w_shard):
         matrices = (g_embed, g_attn, g_ffn_in, g_ffn_out)
         grads = [to_tiles(g[0] if g.ndim == 3 else g[0, 0]) for g in matrices]
-        grads.append(jnp.pad(g_vec, ((0, 0), (0, 0), (0, VEC_BLOCK_ROWS * LANES - VEC_WIDTH))).reshape(VEC_BLOCK_ROWS, LANES))
+        grads.append(g_vec.reshape(1, -1))
         mean_tiles, edges = scatter(grads, m_shard, v_shard, w_shard)
         m_new, v_new, w_new, w_own = mid(mean_tiles, m_shard, v_shard, w_shard, edges)
         full = gather(w_own).reshape(SIXTEEN, OWN, LANES)

time: 337 us -> 335 us (level)
  no operation moved by 1% of the time
where the time goes in v9:
time: 335 us; the launch traced here: 334 us
  Pallas kernels  333 us (99%)
    pallas_call x1, Pallas kernels, scatter(): pl.pallas_call(scatter_kernel, out_shape=(jax.ShapeDtypeStruct((WINDOW, L...  204 us
    pallas_call x1, Pallas kernels, gather(): pl.pallas_call(gather_kernel, out_shape=jax.ShapeDtypeStruct((2, 2, 2, 2,...  103 us
    pallas_call x1, Pallas kernels, mid(): pl.pallas_call(mid_kernel, out_shape=(shard, shard, shard, jax.ShapeDtype...  14 us
    pallas_call x1, Pallas kernels, finish(): pl.pallas_call(final_kernel, out_shape=tuple((shape(end - base) for base,...  12.3 us

profile of v9, /device:TPU:0, one launch (start us, length us, event | category | flops | bytes accessed | tf_op | source)
XLA Modules:
  0.0 334.3 jit_solution(2516112262365199124)
XLA Ops:
  0.6 203.6 %shard_map.151 = (f32[7296,128]{1,0:T(8,128)}, f32[98304]{0:T(1024)}) custom-call(f32[32768,128]{1,0:T(8,128)} %bitcast.43, f32[32768,128]{1,0:T(8,128)} %bitcast.44, f32[22528,128]{1,0:T(8,128)} %bitcast.45, f32[22528,128]{1,0:T(8,128)} %bitcast.46, f32[1,12032]{1,0:T(1,128)} %bitcast.47, f32[885488]{0:T(1024)} %m_ref.3, f32[885488]{0:T(1024)} %v_ref.3, ...), custom_call_target="tpu_custom_call" | custom-call | tf_op jit(solution)/shard_map/pallas_call | solution.py:371
  204.3 0.0 copy-start
  204.3 1.0 copy-done
  205.3 14.0 %shard_map.152 = (f32[885488]{0:T(1024)}, f32[885488]{0:T(1024)}, f32[885488]{0:T(1024)}, bf16[7104,128]{1,0:T(8,128)(2,1)S(1)}) custom-call(f32[7296,128]{1,0:T(8,128)} %get-tuple-element.21.tile_ref, f32[885488]{0:T(1024)} %m_ref.3, f32[885488]{0:T(1024)} %v_ref.3, f32[885488]{0:T(1024)} %w_ref.3, f32[98304]{0:T(1024)S(1)} %copy-done), custom_call_target="tpu_custom_call" | custom-call | tf_op jit(solution)/shard_map/pallas_call | solution.py:652
  219.3 102.6 %shard_map.153 = bf16[2,2,2,2,7104,128]{5,4,3,2,1,0:T(8,128)(2,1)S(1)} custom-call(bf16[7104,128]{1,0:T(8,128)(2,1)S(1)} %get-tuple-element.26.w_ref), custom_call_target="tpu_custom_call" | custom-call | tf_op jit(solution)/shard_map/pallas_call | solution.py:487
  321.9 12.3 %shard_map.154 = (bf16[32768,128]{1,0:T(8,128)(2,1)}, bf16[32768,128]{1,0:T(8,128)(2,1)}, bf16[22528,128]{1,0:T(8,128)(2,1)}, bf16[22528,128]{1,0:T(8,128)(2,1)}...) custom-call(bf16[16,7104,128]{2,1,0:T(8,128)(2,1)S(1)} %bitcast.42), custom_call_target="tpu_custom_call" | custom-call | tf_op jit(solution)/shard_map/pallas_call | solution.py:769
Async XLA Ops:
  204.3 1.0 copy-start

commit v10 on v9

--- a/solution.py
+++ b/solution.py
@@ -534,9 +534,9 @@
     return lax.broadcasted_iota(jnp.int32, (rows, LANES), 1)
 
 
-BATCH = 256
+BATCH = 384
 BATCHES = SHARD_VREGS * 8 // BATCH
-CHUNK_BATCHES = 3
+CHUNK_BATCHES = 2
 CHUNKS = BATCHES // CHUNK_BATCHES
 CHUNK = CHUNK_BATCHES * BATCH * LANES
 
@@ -656,7 +656,7 @@
         scratch_shapes=[
             pltpu.VMEM((SLICE,), jnp.float32), pltpu.VMEM((SLICE,), jnp.float32), pltpu.VMEM((SLICE,), jnp.float32),
             pltpu.VMEM((FLAT_ROWS, LANES), jnp.float32),
-            pltpu.VMEM((PAD + SHARD_VREGS * 8 + 8 + 512, LANES), jnp.float32),
+            pltpu.VMEM((PAD + SHARD_VREGS * 8 + 8 + 640, LANES), jnp.float32),
             pltpu.VMEM((PAD + EDGE_ROWS, LANES), jnp.float32),
             pltpu.VMEM((OWN_FLAT_ROWS, LANES), jnp.float32),
             pltpu.SemaphoreType.DMA((3, CHUNKS)), pltpu.SemaphoreType.DMA((3, CHUNKS)),

time: 335 us -> 333 us (level)
  no operation moved by 1% of the time
where the time goes in v10:
time: 333 us
  Pallas kernels  331 us (99%)
    pallas_call x1, Pallas kernels, scatter(): pl.pallas_call(scatter_kernel, out_shape=(jax.ShapeDtypeStruct((WINDOW, L...  204 us
    pallas_call x1, Pallas kernels, gather(): pl.pallas_call(gather_kernel, out_shape=jax.ShapeDtypeStruct((2, 2, 2, 2,...  103 us
    pallas_call x1, Pallas kernels, mid(): pl.pallas_call(mid_kernel, out_shape=(shard, shard, shard, jax.ShapeDtype...  12.9 us
    pallas_call x1, Pallas kernels, finish(): pl.pallas_call(final_kernel, out_shape=tuple((shape(end - base) for base,...  12.3 us

profile of v10, /device:TPU:0, one launch (start us, length us, event | category | flops | bytes accessed | tf_op | source)
XLA Modules:
  0.0 333.1 jit_solution(2124304018675924133)
XLA Ops:
  0.6 203.6 %shard_map.151 = (f32[7296,128]{1,0:T(8,128)}, f32[98304]{0:T(1024)}) custom-call(f32[32768,128]{1,0:T(8,128)} %bitcast.43, f32[32768,128]{1,0:T(8,128)} %bitcast.44, f32[22528,128]{1,0:T(8,128)} %bitcast.45, f32[22528,128]{1,0:T(8,128)} %bitcast.46, f32[1,12032]{1,0:T(1,128)} %bitcast.47, f32[885488]{0:T(1024)} %m_ref.3, f32[885488]{0:T(1024)} %v_ref.3, ...), custom_call_target="tpu_custom_call" | custom-call | tf_op jit(solution)/shard_map/pallas_call | solution.py:371
  204.3 0.0 copy-start
  204.3 1.0 copy-done
  205.3 12.9 %shard_map.152 = (f32[885488]{0:T(1024)}, f32[885488]{0:T(1024)}, f32[885488]{0:T(1024)}, bf16[7104,128]{1,0:T(8,128)(2,1)S(1)}) custom-call(f32[7296,128]{1,0:T(8,128)} %get-tuple-element.21.tile_ref, f32[885488]{0:T(1024)} %m_ref.3, f32[885488]{0:T(1024)} %v_ref.3, f32[885488]{0:T(1024)} %w_ref.3, f32[98304]{0:T(1024)S(1)} %copy-done), custom_call_target="tpu_custom_call" | custom-call | tf_op jit(solution)/shard_map/pallas_call | solution.py:652
  218.2 102.6 %shard_map.153 = bf16[2,2,2,2,7104,128]{5,4,3,2,1,0:T(8,128)(2,1)S(1)} custom-call(bf16[7104,128]{1,0:T(8,128)(2,1)S(1)} %get-tuple-element.26.w_ref), custom_call_target="tpu_custom_call" | custom-call | tf_op jit(solution)/shard_map/pallas_call | solution.py:487
  320.8 12.3 %shard_map.154 = (bf16[32768,128]{1,0:T(8,128)(2,1)}, bf16[32768,128]{1,0:T(8,128)(2,1)}, bf16[22528,128]{1,0:T(8,128)(2,1)}, bf16[22528,128]{1,0:T(8,128)(2,1)}...) custom-call(bf16[16,7104,128]{2,1,0:T(8,128)(2,1)S(1)} %bitcast.42), custom_call_target="tpu_custom_call" | custom-call | tf_op jit(solution)/shard_map/pallas_call | solution.py:769
Async XLA Ops:
  204.3 1.0 copy-start
